TPU v7x, 128 devices: a whole 4x4x4 slice. The times are simulated.
128 devices in a mesh: tok: 16 (over z, x), mp: 8 (over y, core).
Axes of the slice: x: 4, y: 4, z: 4, core: 2. Of those that a mesh axis runs over, the one named last changes fastest.
Arguments:
- tokens: bfloat16 [6144, 2048], P('tok', 'mp'), may hold values from -120 to 120
- norm_gain: float32 [2048], replicated, may hold values from 0.5 to 1.5
- running_sq: float32 [2048], P('mp'), may hold values from 0.5 to 4
- gate_weight: bfloat16 [2048, 8192], P(None, 'mp'), may hold values from -0.125 to 0.125
- up_weight: bfloat16 [2048, 8192], P(None, 'mp'), may hold values from -0.125 to 0.125
- down_weight_t: bfloat16 [2048, 8192], P(None, 'mp'), may hold values from -0.0625 to 0.0625
- groups: int32 [384], P('tok'), may hold values from 0 to 47, as said below
- cotangent: bfloat16 [6144, 2048], P('tok', 'mp'), may hold values from -6 to 6
Outputs:
- block_out: bfloat16 [6144, 2048], P('tok', 'mp')
- grad_tokens: bfloat16 [6144, 2048], P('tok', 'mp')
- running_new: float32 [2048], P('mp')
- grad_gain: float32 [2048], P('mp')
- grad_gate: float32 [2048, 8192], P('tok', 'mp')
- grad_up: float32 [2048, 8192], P('tok', 'mp')
- grad_down_t: float32 [2048, 8192], P('tok', 'mp')
Inputs may be any that keep to these rules, and one draw needn't show every extreme that they name: Each of the 48 ghost groups holds exactly 8 blocks.
All inputs are finite; a program needn't handle non-finite values.
Results may differ from a plain program's by a relative error of at most 0.02.
Values may be sent and summed in bfloat16 or wider, within the bound.
A program may use at most 128 MiB of HBM per device.

v0:
```python
import jax
import jax.numpy as jnp
from jax import lax
from jax.sharding import PartitionSpec as P

GHOST = 128
BLK = 16


epsilon = 1e-05
momentum = 0.1
highest = lax.Precision.HIGHEST


def from_everyone(x, axis):
    copies = jnp.broadcast_to(x, (lax.axis_size(axis), *x.shape))
    return lax.all_to_all(copies, axis, split_axis=0, concat_axis=0, tiled=True)


def of_everyone(x, axis):
    everything = from_everyone(x, axis)
    return jnp.sum(everything, axis=0)


def laid_out(pieces, dim):
    pieces = jnp.moveaxis(pieces, 0, dim)
    lengths = pieces.shape
    return pieces.reshape(*lengths[:dim], lengths[dim] * lengths[dim + 1], *lengths[dim + 2 :])


def gathered_copies(x, axis, dim):
    return laid_out(from_everyone(x, axis), dim)


def split_up(x, dim, count):
    before, after = (x.shape[:dim], x.shape[dim + 1 :])
    return jnp.moveaxis(x.reshape(*before, count, -1, *after), dim, 0)


def sent_and_summed(x, axis, dim):
    count = lax.axis_size(axis)
    pieces = lax.all_to_all(split_up(x, dim, count), axis, 0, 0, tiled=True)
    return jnp.sum(pieces.astype(jnp.float32), axis=0)


def of_everyone_2(x, axis):
    everything = from_everyone(x, axis)
    return jnp.sum(everything.astype(jnp.float32), axis=0)


def group_sums(values, onehot):
    blocks = values.reshape(values.shape[0] // BLK, BLK, values.shape[1]).sum(axis=1)
    return jnp.dot(onehot, blocks, precision=highest, preferred_element_type=jnp.float32)


def per_token(table, onehot):
    per_block = jnp.dot(onehot.T, table, precision=highest, preferred_element_type=jnp.float32)
    wide = jnp.broadcast_to(per_block[:, None, :], (per_block.shape[0], BLK, per_block.shape[1]))
    return wide.reshape(per_block.shape[0] * BLK, per_block.shape[1])


def contract_rows(left, right):
    return lax.dot_general(
        left, right, (((0,), (0,)), ((), ())), preferred_element_type=jnp.float32
    )


def contract_cols(left, right):
    return lax.dot_general(
        left, right, (((1,), (1,)), ((), ())), preferred_element_type=jnp.float32
    )


def body(tokens, norm_gain, running_sq, gate_weight, up_weight, down_weight_t, groups, cotangent):
    tok_count = lax.axis_size("tok")
    tok_rows, feat_width = tokens.shape
    groups_total = tok_rows * tok_count // GHOST
    onehot = (groups[None, :] == jnp.arange(groups_total, dtype=jnp.int32)[:, None]).astype(
        jnp.float32
    )
    col_first = lax.axis_index("mp") * feat_width
    x_local = tokens.astype(jnp.float32)
    gain_local = lax.dynamic_slice_in_dim(norm_gain, col_first, feat_width, 0)
    quad_mean = of_everyone(group_sums(x_local * x_local, onehot), "tok") / GHOST
    scale = per_token(lax.rsqrt(quad_mean + epsilon), onehot)
    normed = x_local * scale
    hid_in = gathered_copies((gain_local * normed).astype(jnp.bfloat16), "mp", 1)
    dy_full = gathered_copies(cotangent, "mp", 1)
    gate = jnp.dot(hid_in, gate_weight, preferred_element_type=jnp.float32)
    lift = jnp.dot(hid_in, up_weight, preferred_element_type=jnp.float32)
    sigma = jax.nn.sigmoid(gate)
    hidden = (gate * sigma * lift).astype(jnp.bfloat16)
    branch = sent_and_summed(contract_cols(hidden, down_weight_t).astype(jnp.bfloat16), "mp", 1)
    block_out = (x_local + branch).astype(jnp.bfloat16)
    running_new = (1.0 - momentum) * running_sq + momentum * jnp.mean(quad_mean, axis=0)
    grad_hidden = jnp.dot(dy_full, down_weight_t, preferred_element_type=jnp.float32)
    grad_gate_in = (grad_hidden * lift * sigma * (1.0 + gate * (1.0 - sigma))).astype(jnp.bfloat16)
    grad_lift = (grad_hidden * gate * sigma).astype(jnp.bfloat16)
    grad_partial = contract_cols(grad_gate_in, gate_weight) + contract_cols(grad_lift, up_weight)
    grad_normed_in = sent_and_summed(grad_partial.astype(jnp.bfloat16), "mp", 1)
    partial_value = of_everyone_2(
        group_sums(grad_normed_in * normed, onehot).astype(jnp.bfloat16), "tok"
    ).astype(jnp.float32)
    grad_gain = jnp.sum(partial_value, axis=0)
    mean_term = per_token(gain_local * partial_value / GHOST, onehot)
    grad_tokens = (
        cotangent.astype(jnp.float32) + scale * (gain_local * grad_normed_in - normed * mean_term)
    ).astype(jnp.bfloat16)
    both_grads = jnp.concatenate([grad_gate_in, grad_lift], axis=1)
    hidden_width = gate_weight.shape[1]
    upper = contract_rows(hid_in, both_grads)
    lower = contract_rows(dy_full, hidden)
    weight_total = lax.psum_scatter(
        jnp.concatenate([upper, lower], axis=1).astype(jnp.bfloat16),
        "tok",
        scatter_dimension=0,
        tiled=True,
    ).astype(jnp.float32)
    grad_gate = weight_total[:, :hidden_width]
    grad_up = weight_total[:, hidden_width : 2 * hidden_width]
    grad_down_t = weight_total[:, 2 * hidden_width :]
    return (block_out, grad_tokens, running_new, grad_gain, grad_gate, grad_up, grad_down_t)


def solution(mesh):
    placed = (
        P("tok", "mp"),
        P(),
        P("mp"),
        P(None, "mp"),
        P(None, "mp"),
        P(None, "mp"),
        P("tok"),
        P("tok", "mp"),
    )
    return jax.shard_map(
        body,
        mesh=mesh,
        in_specs=placed,
        out_specs=(
            P("tok", "mp"),
            P("tok", "mp"),
            P("mp"),
            P("mp"),
            P("tok", "mp"),
            P("tok", "mp"),
            P("tok", "mp"),
        ),
        check_vma=False,
    )
```

profile of v0, /device:TPU:32, one launch (start us, length us, event | category | flops | bytes accessed | tf_op | source)
XLA Modules:
  0.0 231.6 jit_solution(3055635269094535712)
XLA Ops:
  7.2 1.0 convert_multiply_fusion
  8.1 0.1 reduce_sum.72
  8.2 0.8 fusion.22
  9.0 0.0 copy-start.10
  9.0 0.0 copy-start
  9.0 1.0 broadcast_in_dim.12
  10.0 7.9 %all-to-all-start = ((f32[16,48,256]{2,1,0:T(8,128)}), f32[16,48,256]{2,1,0:T(8,128)S(1)}, u32[]{:S(2)}, u32[]{:S(2)}) async-start(f32[16,48,256]{2,1,0:T(8,128)} %broadcast_in_dim.12), calls=%async_computation | async-start | bytes 1572864 | tf_op jit(solution)/shard_map/all_to_all | solution.py:17
  17.9 0.8 dynamic_slice.3
  18.7 11.0 %all-to-all-done = f32[16,48,256]{2,1,0:T(8,128)S(1)} async-done(((f32[16,48,256]{2,1,0:T(8,128)}), f32[16,48,256]{2,1,0:T(8,128)S(1)}, u32[]{:S(2)}, u32[]{:S(2)}) %all-to-all-start) | async-done | bytes 786464 | tf_op jit(solution)/shard_map/all_to_all | solution.py:17
  29.7 0.1 reduce_sum.73
  29.7 0.0 copy-start.5
  29.7 0.2 fusion.14
  29.9 0.0 copy-start.7
  30.0 0.1 fusion.6
  30.0 0.2 copy.30
  30.2 1.3 broadcast_in_dim.14
  31.5 0.0 copy-done.5
  31.5 4.6 %all-to-all-start.1 = ((bf16[8,384,256]{1,2,0:T(8,128)(2,1)}), bf16[8,384,256]{1,2,0:T(8,128)(2,1)S(1)}, u32[]{:S(2)}, u32[]{:S(2)}) async-start(bf16[8,384,256]{1,2,0:T(8,128)(2,1)} %broadcast_in_dim.14), calls=%async_computation.1 | async-start | bytes 3145728 | tf_op jit(solution)/shard_map/all_to_all | solution.py:17
  36.1 0.2 copy.32
  36.3 21.4 %all-to-all-done.1 = bf16[8,384,256]{1,2,0:T(8,128)(2,1)S(1)} async-done(((bf16[8,384,256]{1,2,0:T(8,128)(2,1)}), bf16[8,384,256]{1,2,0:T(8,128)(2,1)S(1)}, u32[]{:S(2)}, u32[]{:S(2)}) %all-to-all-start.1) | async-done | bytes 1572896 | tf_op jit(solution)/shard_map/all_to_all | solution.py:17
  57.7 1.3 broadcast_in_dim.15
  58.9 3.6 %all-to-all-start.3 = ((bf16[8,384,256]{1,2,0:T(8,128)(2,1)}), bf16[8,384,256]{1,2,0:T(8,128)(2,1)S(1)}, u32[]{:S(2)}, u32[]{:S(2)}) async-start(bf16[8,384,256]{1,2,0:T(8,128)(2,1)} %broadcast_in_dim.15), calls=%async_computation.3 | async-start | bytes 3145728 | tf_op jit(solution)/shard_map/all_to_all | solution.py:17
  62.5 0.0 reduce-scatter.4.cloned.1.call-start
  62.6 0.0 copy-start.12
  62.6 5.3 %fusion.33 = f32[384,1024]{1,0:T(8,128)} fusion(bf16[384,2048]{0,1:T(8,128)(2,1)S(1)} %bitcast.63, bf16[2048,1024]{1,0:T(8,128)(2,1)} %param.12), kind=kOutput, calls=%fused_computation.56 | convolution fusion | flops 1610612736 | bytes 7340032 | tf_op jit(solution)/shard_map/dot_general | solution.py:90
  67.9 3.0 %fusion.32 = f32[384,1024]{1,0:T(8,128)} fusion(bf16[384,2048]{0,1:T(8,128)(2,1)S(1)} %bitcast.64, bf16[2048,1024]{1,0:T(8,128)(2,1)S(1)} %copy-done.12), kind=kOutput, calls=%fused_computation.55 | convolution fusion | flops 1610612736 | bytes 7340032 | tf_op jit(solution)/shard_map/dot_general | solution.py:89
  70.9 13.1 %all-to-all-done.3 = bf16[8,384,256]{1,2,0:T(8,128)(2,1)S(1)} async-done(((bf16[8,384,256]{1,2,0:T(8,128)(2,1)}), bf16[8,384,256]{1,2,0:T(8,128)(2,1)S(1)}, u32[]{:S(2)}, u32[]{:S(2)}) %all-to-all-start.3) | async-done | bytes 1572896 | tf_op jit(solution)/shard_map/all_to_all | solution.py:17
  84.0 5.5 %multiply_convert_fusion = (bf16[384,1024]{1,0:T(8,128)(2,1)S(1)}, bf16[384,1024]{1,0:T(8,128)(2,1)S(1)}, bf16[384,1024]{1,0:T(8,128)(2,1)S(1)}) fusion(f32[384,1024]{1,0:T(8,128)} %fusion.32, f32[384,1024]{1,0:T(8,128)} %fusion.33, bf16[384,2048]{0,1:T(8,128)(2,1)S(1)} %bitcast.66, bf16[2048,1024]{1,0:T(8,128)(2,1)} %param.13), kind=kOutput, calls=%fused_computation.12 | convolution fusion | flops 1616904192 | bytes 11272192 | tf_op jit(solution)/shard_map/dot_general | solution.py:96
  89.6 2.4 %convert_bitcast_fusion = bf16[2048,1024]{0,1:T(8,128)(2,1)S(1)} fusion(bf16[384,1024]{1,0:T(8,128)(2,1)S(1)} %get-tuple-element.39, bf16[384,2048]{0,1:T(8,128)(2,1)S(1)} %bitcast.67), kind=kOutput, calls=%fused_computation.2 | convolution fusion | flops 1612709888 | bytes 6553600 | tf_op jit(solution)/shard_map/dot_general | solution.py:63
  92.0 5.1 %convolution_convert_fusion = bf16[2048,2048]{0,1:T(8,128)(2,1)S(1)} fusion(bf16[384,2048]{0,1:T(8,128)(2,1)S(1)} %bitcast.65, bf16[384,1024]{1,0:T(8,128)(2,1)S(1)} %get-tuple-element.37, bf16[384,1024]{1,0:T(8,128)(2,1)S(1)} %get-tuple-element.38), kind=kOutput, calls=%fused_computation.1 | convolution fusion | flops 3228565504 | bytes 11534336 | tf_op jit(solution)/shard_map/dot_general | solution.py:63
  97.1 14.4 %pad_maximum_fusion = bf16[2048,3072]{0,1:T(8,128)(2,1)} fusion(bf16[2048,1024]{0,1:T(8,128)(2,1)S(1)} %convert_bitcast_fusion, bf16[2048,2048]{0,1:T(8,128)(2,1)S(1)} %convolution_convert_fusion), kind=kLoop, calls=%fused_computation | loop fusion | flops 25165824 | bytes 25165824 | tf_op jit(solution)/shard_map/concatenate | solution.py:114
  111.4 16.6 %copy.37 = bf16[2048,3072]{1,0:T(8,128)(2,1)} copy(bf16[2048,3072]{0,1:T(8,128)(2,1)} %pad_maximum_fusion) | data formatting | bytes 25165824
  128.1 0.0 reduce-scatter.4.cloned.1.call-update
  128.1 1.1 copy-done.15
  129.2 4.2 %fusion.34 = f32[384,2048]{1,0:T(8,128)S(1)} fusion(bf16[384,1024]{1,0:T(8,128)(2,1)S(1)} %copy-done.15, bf16[2048,1024]{1,0:T(8,128)(2,1)} %param.11), kind=kOutput, calls=%fused_computation.57 | convolution fusion | flops 1610612736 | bytes 8126464 | tf_op jit(solution)/shard_map/dot_general | solution.py:69
  133.4 1.8 add_convert_fusion
  135.2 1.3 copy.43
  136.5 3.7 %all-to-all-start.4 = ((bf16[8,384,256]{2,1,0:T(8,128)(2,1)}), bf16[8,384,256]{2,1,0:T(8,128)(2,1)S(1)}, u32[]{:S(2)}, u32[]{:S(2)}) async-start(bf16[8,384,256]{2,1,0:T(8,128)(2,1)} %bitcast.60), calls=%async_computation.4 | async-start | bytes 3145728 | tf_op jit(solution)/shard_map/all_to_all | solution.py:42
  140.3 4.1 %convolution_convert_fusion.1 = bf16[384,2048]{1,0:T(8,128)(2,1)S(1)} fusion(bf16[384,1024]{1,0:T(8,128)(2,1)S(1)} %copy-done.17, bf16[2048,1024]{1,0:T(8,128)(2,1)} %param.13), kind=kOutput, calls=%fused_computation.6 | convolution fusion | flops 1611399168 | bytes 6553600 | tf_op jit(solution)/shard_map/dot_general | solution.py:69
  144.4 1.2 copy.44
  145.6 16.1 %all-to-all-done.4 = bf16[8,384,256]{2,1,0:T(8,128)(2,1)S(1)} async-done(((bf16[8,384,256]{2,1,0:T(8,128)(2,1)}), bf16[8,384,256]{2,1,0:T(8,128)(2,1)S(1)}, u32[]{:S(2)}, u32[]{:S(2)}) %all-to-all-start.4) | async-done | bytes 1572896 | tf_op jit(solution)/shard_map/all_to_all | solution.py:42
  161.7 3.7 %all-to-all-start.2 = ((bf16[8,384,256]{2,1,0:T(8,128)(2,1)}), bf16[8,384,256]{2,1,0:T(8,128)(2,1)S(1)}, u32[]{:S(2)}, u32[]{:S(2)}) async-start(bf16[8,384,256]{2,1,0:T(8,128)(2,1)} %bitcast.62), calls=%async_computation.2 | async-start | bytes 3145728 | tf_op jit(solution)/shard_map/all_to_all | solution.py:42
  165.5 0.0 copy-start.1
  165.5 0.0 copy-start.8
  165.5 0.2 convert_reduce_fusion
  165.7 0.7 copy-done.1
  166.4 0.1 fusion.4
  166.5 0.1 reduce_sum.76
  166.6 0.1 convolution_convert_fusion.2
  166.7 20.2 %all-to-all-done.2 = bf16[8,384,256]{2,1,0:T(8,128)(2,1)S(1)} async-done(((bf16[8,384,256]{2,1,0:T(8,128)(2,1)}), bf16[8,384,256]{2,1,0:T(8,128)(2,1)S(1)}, u32[]{:S(2)}, u32[]{:S(2)}) %all-to-all-start.2) | async-done | bytes 1572896 | tf_op jit(solution)/shard_map/all_to_all | solution.py:42
  186.9 0.8 broadcast_in_dim.16
  187.7 6.4 %all-to-all-start.5 = ((bf16[16,48,256]{2,1,0:T(8,128)(2,1)}), bf16[16,48,256]{2,1,0:T(8,128)(2,1)S(1)}, u32[]{:S(2)}, u32[]{:S(2)}) async-start(bf16[16,48,256]{2,1,0:T(8,128)(2,1)} %broadcast_in_dim.16), calls=%async_computation.5 | async-start | bytes 786432 | tf_op jit(solution)/shard_map/all_to_all | solution.py:17
  194.1 0.6 multiply_add_fusion
  194.6 0.2 convert_reduce_fusion.1
  194.9 7.2 %all-to-all-done.5 = bf16[16,48,256]{2,1,0:T(8,128)(2,1)S(1)} async-done(((bf16[16,48,256]{2,1,0:T(8,128)(2,1)}), bf16[16,48,256]{2,1,0:T(8,128)(2,1)S(1)}, u32[]{:S(2)}, u32[]{:S(2)}) %all-to-all-start.5) | async-done | bytes 393248 | tf_op jit(solution)/shard_map/all_to_all | solution.py:17
  202.1 0.7 convert_reduce_fusion.2
  202.8 0.2 fusion.11
  203.0 0.9 fusion.10
  203.9 16.3 %reduce-scatter.4.cloned.1.call-done = bf16[128,3072]{1,0:T(8,128)(2,1)} async-done(((bf16[2048,3072]{1,0:T(8,128)(2,1)}), bf16[128,3072]{1,0:T(8,128)(2,1)}) %reduce-scatter.4.cloned.1.call-update) | async-done | bytes 786448
  220.2 1.5 copy.38
  221.7 0.1 fusion.31
  221.8 1.0 copy.36
  222.8 1.0 copy.35
  223.8 1.0 copy.34
  (31 shorter events, 0.1 us)
Async XLA Ops:
  9.0 20.7 %copy-start.10 = (s32[24]{0:T(128)S(1)}, s32[24]{0:T(128)}, u32[]{:S(2)}) copy-start(s32[24]{0:T(128)} %param.14) | copy-start | bytes 292
  9.0 20.9 %copy-start = (bf16[384,256]{1,0:T(8,128)(2,1)S(1)}, bf16[384,256]{1,0:T(8,128)(2,1)}, u32[]{:S(2)}) copy-start(bf16[384,256]{1,0:T(8,128)(2,1)} %param.8) | copy-start | bytes 589828
  10.0 19.7 %all-to-all-start = ((f32[16,48,256]{2,1,0:T(8,128)}), f32[16,48,256]{2,1,0:T(8,128)S(1)}, u32[]{:S(2)}, u32[]{:S(2)}) async-start(f32[16,48,256]{2,1,0:T(8,128)} %broadcast_in_dim.12), calls=%async_computation | async-start | bytes 1572864 | tf_op jit(solution)/shard_map/all_to_all | solution.py:17
  29.7 1.8 copy-start.5
  29.9 1.6 copy-start.7
  31.5 4.6 %copy-start.3 = (bf16[384,256]{1,0:T(8,128)(2,1)S(1)}, bf16[384,256]{1,0:T(8,128)(2,1)}, u32[]{:S(2)}) copy-start(bf16[384,256]{1,0:T(8,128)(2,1)} %param.15) | copy-start | bytes 589828
  31.5 26.2 %all-to-all-start.1 = ((bf16[8,384,256]{1,2,0:T(8,128)(2,1)}), bf16[8,384,256]{1,2,0:T(8,128)(2,1)S(1)}, u32[]{:S(2)}, u32[]{:S(2)}) async-start(bf16[8,384,256]{1,2,0:T(8,128)(2,1)} %broadcast_in_dim.14), calls=%async_computation.1 | async-start | bytes 3145728 | tf_op jit(solution)/shard_map/all_to_all | solution.py:17
  58.9 25.1 %all-to-all-start.3 = ((bf16[8,384,256]{1,2,0:T(8,128)(2,1)}), bf16[8,384,256]{1,2,0:T(8,128)(2,1)S(1)}, u32[]{:S(2)}, u32[]{:S(2)}) async-start(bf16[8,384,256]{1,2,0:T(8,128)(2,1)} %broadcast_in_dim.15), calls=%async_computation.3 | async-start | bytes 3145728 | tf_op jit(solution)/shard_map/all_to_all | solution.py:17
  62.5 157.7 %reduce-scatter.4.cloned.1.call-start = ((), (), s32[]{:S(2)}) async-start(), calls=%async_computation.7 | async-start | bytes 13369344
  62.6 5.4 %copy-start.12 = (bf16[2048,1024]{1,0:T(8,128)(2,1)S(1)}, bf16[2048,1024]{1,0:T(8,128)(2,1)}, u32[]{:S(2)}) copy-start(bf16[2048,1024]{1,0:T(8,128)(2,1)} %param.11) | copy-start | bytes 12582916
  89.6 2.4 %copy-start.16 = (bf16[384,1024]{1,0:T(8,128)(2,1)}, bf16[384,1024]{1,0:T(8,128)(2,1)S(1)}, u32[]{:S(2)}) copy-start(bf16[384,1024]{1,0:T(8,128)(2,1)S(1)} %get-tuple-element.39) | copy-start | bytes 2359300
  89.6 2.4 %copy-start.14 = (bf16[384,1024]{1,0:T(8,128)(2,1)}, bf16[384,1024]{1,0:T(8,128)(2,1)S(1)}, u32[]{:S(2)}) copy-start(bf16[384,1024]{1,0:T(8,128)(2,1)S(1)} %get-tuple-element.38) | copy-start | bytes 2359300
  89.6 2.4 %copy-start.18 = (bf16[384,1024]{1,0:T(8,128)(2,1)}, bf16[384,1024]{1,0:T(8,128)(2,1)S(1)}, u32[]{:S(2)}) copy-start(bf16[384,1024]{1,0:T(8,128)(2,1)S(1)} %get-tuple-element.37) | copy-start | bytes 2359300
  128.1 1.1 copy-start.15
  129.2 4.2 %copy-start.13 = (bf16[2048,1024]{1,0:T(8,128)(2,1)S(1)}, bf16[2048,1024]{1,0:T(8,128)(2,1)}, u32[]{:S(2)}) copy-start(bf16[2048,1024]{1,0:T(8,128)(2,1)} %param.12) | copy-start | bytes 12582916
  129.2 4.2 %copy-start.19 = (bf16[384,1024]{1,0:T(8,128)(2,1)S(1)}, bf16[384,1024]{1,0:T(8,128)(2,1)}, u32[]{:S(2)}) copy-start(bf16[384,1024]{1,0:T(8,128)(2,1)} %copy-done.18) | copy-start | bytes 2359300
  136.5 3.7 %copy-start.17 = (bf16[384,1024]{1,0:T(8,128)(2,1)S(1)}, bf16[384,1024]{1,0:T(8,128)(2,1)}, u32[]{:S(2)}) copy-start(bf16[384,1024]{1,0:T(8,128)(2,1)} %copy-done.16) | copy-start | bytes 2359300
  136.5 25.2 %all-to-all-start.4 = ((bf16[8,384,256]{2,1,0:T(8,128)(2,1)}), bf16[8,384,256]{2,1,0:T(8,128)(2,1)S(1)}, u32[]{:S(2)}, u32[]{:S(2)}) async-start(bf16[8,384,256]{2,1,0:T(8,128)(2,1)} %bitcast.60), calls=%async_computation.4 | async-start | bytes 3145728 | tf_op jit(solution)/shard_map/all_to_all | solution.py:42
  161.7 3.7 %copy-start.6 = (f32[48,256]{1,0:T(8,128)S(1)}, f32[48,256]{1,0:T(8,128)}, u32[]{:S(2)}) copy-start(f32[48,256]{1,0:T(8,128)} %copy-done.5) | copy-start | bytes 147460
  161.7 25.2 %all-to-all-start.2 = ((bf16[8,384,256]{2,1,0:T(8,128)(2,1)}), bf16[8,384,256]{2,1,0:T(8,128)(2,1)S(1)}, u32[]{:S(2)}, u32[]{:S(2)}) async-start(bf16[8,384,256]{2,1,0:T(8,128)(2,1)} %bitcast.62), calls=%async_computation.2 | async-start | bytes 3145728 | tf_op jit(solution)/shard_map/all_to_all | solution.py:42
  165.5 0.9 copy-start.1
  165.5 0.9 copy-start.8
  166.4 27.7 %copy-start.11 = (f32[256]{0:T(256)S(1)}, f32[256]{0:T(256)}, u32[]{:S(2)}) copy-start(f32[256]{0:T(256)} %param.10) | copy-start | bytes 3076
  187.7 15.3 %copy-start.2 = (bf16[384,256]{1,0:T(8,128)(2,1)S(1)}, bf16[384,256]{1,0:T(8,128)(2,1)}, u32[]{:S(2)}) copy-start(bf16[384,256]{1,0:T(8,128)(2,1)} %param.8) | copy-start | bytes 589828
  187.7 15.3 %copy-start.4 = (bf16[384,256]{1,0:T(8,128)(2,1)S(1)}, bf16[384,256]{1,0:T(8,128)(2,1)}, u32[]{:S(2)}) copy-start(bf16[384,256]{1,0:T(8,128)(2,1)} %param.15) | copy-start | bytes 589828
  187.7 15.3 %copy-start.9 = (f32[24,256]{1,0:T(8,128)S(1)}, f32[24,256]{1,0:T(8,128)}, u32[]{:S(2)}) copy-start(f32[24,256]{1,0:T(8,128)} %copy-done.7) | copy-start | bytes 73732
  187.7 14.4 %all-to-all-start.5 = ((bf16[16,48,256]{2,1,0:T(8,128)(2,1)}), bf16[16,48,256]{2,1,0:T(8,128)(2,1)S(1)}, u32[]{:S(2)}, u32[]{:S(2)}) async-start(bf16[16,48,256]{2,1,0:T(8,128)(2,1)} %broadcast_in_dim.16), calls=%async_computation.5 | async-start | bytes 786432 | tf_op jit(solution)/shard_map/all_to_all | solution.py:17
Sparse Core Ops, SparseCore 0:
  128.2 91.9 reduce-scatter.3
where the time goes:
time: 234 us; the launch traced here: 232 us
  waiting for transfers between devices  105 us (45%)
  matrix products  32.8 us (14%)
  local copies, waits for them, and re-layouts  31 us (13%)
  starting transfers between devices  29.9 us (13%)
  other arithmetic  18.2 us (8%)
  between operations  14.4 us (6%)
    all_to_all x4, waiting for transfers between devices, from_everyone(): return lax.all_to_all(copies, axis, split_axis=0, concat_axis=0, tiled=True)  52.6 us
    all_to_all x2, waiting for transfers between devices, sent_and_summed(): pieces = lax.all_to_all(split_up(x, dim, count), axis, 0, 0, tiled=True)  36.3 us
    unnamed x46, local copies, waits for them, and re-layouts  23.2 us
    all_to_all x4, starting transfers between devices, from_everyone(): return lax.all_to_all(copies, axis, split_axis=0, concat_axis=0, tiled=True)  22.4 us
    unnamed x2, waiting for transfers between devices  16.3 us
    concatenate x1, other arithmetic, body(): jnp.concatenate([upper, lower], axis=1).astype(jnp.bfloat16)  14.4 us
    dot_general x3, matrix products, contract_cols(): lax.dot_general(left, right, (((1,), (1,)), ((), ())), preferred_element_...  10.1 us
    dot_general x2, matrix products, contract_rows(): lax.dot_general(left, right, (((0,), (0,)), ((), ())), preferred_element_...  7.46 us
  transfers between devices with their start and end apart: 7, of which 7 were waited for; matrix products, arithmetic and copies ran while one was open for 11% of the time, Pallas kernels for 0%

commit v1 on v0

v1 whole, which is shorter than its diff:
```python
import jax
import jax.numpy as jnp
from jax import lax
from jax.experimental import pallas as pl
from jax.experimental.pallas import tpu as pltpu
from jax.sharding import PartitionSpec as P

GHOST = 128
BLK = 16
ROWS = 384
FEAT = 256
WIDTH = 2048
HALF = 512
GROUPS = 48
NB = 24
TOK = 16
PIECES = 6

epsilon = 1e-05
momentum = 0.1
F32 = jnp.float32
BF16 = jnp.bfloat16
HIGHEST = lax.Precision.HIGHEST


def kernel(
    tok_hbm, gain_ref, run_ref, gw_hbm, uw_hbm, dw_hbm, grp_ref, cot_hbm,
    bo_ref, gt_ref, rn_ref, gg_ref, gr_ref,
    XT, NRM, BSUM, SCB, DYB, HB, LT, W, G, GT, LF, GH,
    SB, PS, PA, RSA, SPA, QA, R1, R2, PB, T1, T2, BK, BS, U1, BP, U2,
    EK, ES, ER, V1, V2, WS, W1, FS,
    lsem, gsend, grecv, ssend, srecv, wsend, wrecv, ysend, yrecv,
):
    t = lax.axis_index("tok")
    m = lax.axis_index("mp")
    z, x = t // 4, t % 4
    y, c = m // 2, m % 2
    zp = z + 1 - 2 * (z % 2)
    zs = 3 - z
    role = ((z + 1) // 2) % 2
    yp, ym, y2 = (y + 1) % 4, (y + 3) % 4, (y + 2) % 4
    xp, xm, x2 = (x + 1) % 4, (x + 3) % 4, (x + 2) % 4
    dC = (t, y * 2 + 1 - c)
    dP = (zp * 4 + x, m)
    dS = (zs * 4 + x, m)
    dYp, dYm = (t, yp * 2 + c), (t, ym * 2 + c)
    dXp, dXm = (z * 4 + xp, m), (z * 4 + xm, m)

    def rc(src, dst, ss, rs, dev):
        return pltpu.make_async_remote_copy(
            src_ref=src, dst_ref=dst, send_sem=ss, recv_sem=rs,
            device_id=dev, device_id_type=pl.DeviceIdType.MESH,
        )

    own_cols = pl.ds(pl.multiple_of(m * FEAT, FEAT), FEAT)

    cp_dy = pltpu.make_async_copy(cot_hbm, DYB.at[0, :, own_cols], lsem.at[0])
    cp_dy.start()
    cp_x = pltpu.make_async_copy(tok_hbm, XT, lsem.at[1])
    cp_x.start()
    wcols = pl.ds(pl.multiple_of(role * HALF, HALF), HALF)
    cp_w = [
        pltpu.make_async_copy(h.at[:, wcols], W.at[i], lsem.at[2 + i])
        for i, h in enumerate((gw_hbm, uw_hbm, dw_hbm))
    ]
    for k in (2, 0, 1):
        cp_w[k].start()

    bar = pltpu.get_barrier_semaphore()
    for k in range(1, TOK):
        pl.semaphore_signal(
            bar, inc=1, device_id=((t + k) % TOK, m), device_id_type=pl.DeviceIdType.MESH
        )
    for d in (dC, dYp, dYm):
        pl.semaphore_signal(bar, inc=1, device_id=d, device_id_type=pl.DeviceIdType.MESH)
    pl.semaphore_wait(bar, TOK - 1 + 3)

    def sl(B, slot, yy, cc, r0=0, n=ROWS):
        return B.at[slot, pl.ds(r0, n), pl.ds(pl.multiple_of((yy * 2 + cc) * FEAT, FEAT), FEAT)]

    def gcopy(B, g, k):
        h = ROWS // 2
        if k == 0:
            a, b, d = sl(B, 0, y, c), sl(B, 1, y, c), dP
        elif k == 1:
            a = b = sl(B, 0, y, c)
            d = dYp
        elif k == 2:
            a = b = sl(B, 0, y, c)
            d = dYm
        elif k == 3:
            a = b = sl(B, 0, ym, c, 0, h)
            d = dYp
        elif k == 4:
            a = b = sl(B, 0, yp, c, h, h)
            d = dYm
        elif k == 5:
            a = b = sl(B, 1, y, c)
            d = dYp
        elif k == 6:
            a = b = sl(B, 1, y, c)
            d = dYm
        elif k == 7:
            a, b, d = sl(B, 0, y2, c), sl(B, 1, y2, c), dP
        else:
            slot = (k - 8) // 4
            yy = (y, ym, yp, y2)[(k - 8) % 4]
            a = b = sl(B, slot, yy, c)
            d = dC
        return rc(a, b, gsend.at[g, k], grecv.at[g, k], d)

    def gland(B, g, k):
        h = ROWS // 2
        if k == 0:
            b = sl(B, 1, y, c)
        elif k == 1:
            b = sl(B, 0, ym, c)
        elif k == 2:
            b = sl(B, 0, yp, c)
        elif k == 3:
            b = sl(B, 0, y2, c, 0, h)
        elif k == 4:
            b = sl(B, 0, y2, c, h, h)
        elif k == 5:
            b = sl(B, 1, ym, c)
        elif k == 6:
            b = sl(B, 1, yp, c)
        elif k == 7:
            b = sl(B, 1, y2, c)
        else:
            b = sl(B, (k - 8) // 4, (y, ym, yp, y2)[(k - 8) % 4], 1 - c)
        rc(b, b, gsend.at[g, k], grecv.at[g, k], dC).wait_recv()

    def gstart(B, g, *ks):
        for k in ks:
            gcopy(B, g, k).start()

    def fwdA(B, g):
        gland(B, g, 1)
        gstart(B, g, 3, 9)
        gland(B, g, 2)
        gstart(B, g, 4, 10)

    def fwdP(B, g):
        gland(B, g, 0)
        gstart(B, g, 5, 6, 12)

    def fwdB(B, g):
        gland(B, g, 3)
        gland(B, g, 4)
        gstart(B, g, 7, 11)

    def fwdC(B, g):
        gland(B, g, 5)
        gstart(B, g, 13)
        gland(B, g, 6)
        gstart(B, g, 14)

    def fwdD(B, g):
        gland(B, g, 7)
        gstart(B, g, 15)

    def table_send(buf, e):
        for k in range(1, TOK):
            rc(buf.at[t], buf.at[t], ssend.at[e, k], srecv.at[e, k], ((t + k) % TOK, m)).start()

    def table_sum(buf, e):
        for k in range(1, TOK):
            s = (t + TOK - k) % TOK
            rc(buf.at[s], buf.at[s], ssend.at[e, k], srecv.at[e, k], dC).wait_recv()
        total = buf[0].astype(F32)
        for k in range(1, TOK):
            total = total + buf[k].astype(F32)
        return total

    grow = grp_ref[...]
    onehot = (
        lax.broadcasted_iota(jnp.int32, (GROUPS, NB), 0) == jnp.broadcast_to(grow, (GROUPS, NB))
    ).astype(F32)
    diag = lax.broadcasted_iota(jnp.int32, (NB, NB), 0) == lax.broadcasted_iota(
        jnp.int32, (NB, NB), 1
    )
    gcol = jnp.sum(
        jnp.where(diag, jnp.broadcast_to(grow, (NB, NB)), 0).astype(F32), axis=1, keepdims=True
    )
    onehot_t = (
        lax.broadcasted_iota(jnp.int32, (NB, GROUPS), 1).astype(F32)
        == jnp.broadcast_to(gcol, (NB, GROUPS))
    ).astype(F32)

    cp_dy.wait()
    gstart(DYB, 0, 1, 2, 8)
    cp_x.wait()
    for b in range(NB):
        xb = XT[b * BLK : (b + 1) * BLK, :].astype(F32)
        BSUM[b : b + 1, :] = jnp.sum(xb * xb, axis=0, keepdims=True)
    SB[t] = jnp.dot(onehot, BSUM[...], precision=HIGHEST, preferred_element_type=F32).astype(BF16)
    table_send(SB, 0)
    gstart(DYB, 0, 0)
    fwdA(DYB, 0)
    fwdP(DYB, 0)

    quad = table_sum(SB, 0) / GHOST
    rn_ref[...] = (1.0 - momentum) * run_ref[...] + momentum * (
        jnp.sum(quad, axis=0, keepdims=True) / GROUPS
    )
    SCB[...] = jnp.dot(
        onehot_t, lax.rsqrt(quad + epsilon), precision=HIGHEST, preferred_element_type=F32
    )
    gain = gain_ref[:, own_cols]
    for b in range(NB):
        rows = slice(b * BLK, (b + 1) * BLK)
        nb = XT[rows, :].astype(F32) * SCB[b : b + 1, :]
        NRM[rows, :] = nb
        HB[0, rows, own_cols] = (gain * nb).astype(BF16)
    gstart(HB, 1, 1, 2, 8, 0)

    fwdB(DYB, 0)
    fwdC(DYB, 0)
    fwdD(DYB, 0)
    for k in range(8, 16):
        gland(DYB, 0, k)

    def transposed(B, i, slot):
        @pl.loop(0, 8)
        def _(j):
            cols = pl.ds(pl.multiple_of(j * FEAT, FEAT), FEAT)
            LT[i, cols, pl.ds(slot * ROWS, ROWS)] = B[slot, :, cols].T

    def units(slot):
        GT[...] = jnp.dot(HB[slot], W[0], preferred_element_type=F32)
        LF[...] = jnp.dot(HB[slot], W[1], preferred_element_type=F32)

        @pl.loop(0, ROWS // 16)
        def _(i):
            r = pl.ds(pl.multiple_of(i * 16, 16), 16)
            ro = pl.ds(pl.multiple_of(slot * ROWS + i * 16, 16), 16)
            gate, lift, gh = GT[r, :], LF[r, :], GH[slot, r, :]
            sigma = jax.nn.sigmoid(gate)
            G[2, ro, :] = (gate * sigma * lift).astype(BF16)
            G[0, ro, :] = (gh * lift * sigma * (1.0 + gate * (1.0 - sigma))).astype(BF16)
            G[1, ro, :] = (gh * gate * sigma).astype(BF16)

    cp_w[2].wait()
    for s in range(2):
        GH[s] = jnp.dot(DYB[s], W[2], preferred_element_type=F32)
    fwdA(HB, 1)
    fwdP(HB, 1)
    transposed(DYB, 1, 0)
    transposed(DYB, 1, 1)
    fwdB(HB, 1)
    cp_w[0].wait()
    cp_w[1].wait()
    for k in range(8, 12):
        gland(HB, 1, k)
    transposed(HB, 0, 0)
    units(0)
    fwdC(HB, 1)
    fwdD(HB, 1)
    for k in range(12, 16):
        gland(HB, 1, k)
    transposed(HB, 0, 1)
    units(1)

    AS, AP, AX1P, AX1M, AX2P, AX2M, BX1P, BX1M, BX2P, BX2M, BSK, BPK = range(12)

    def wcopy(k, p, src, dst, dev):
        return rc(src, dst, wsend.at[k, p], wrecv.at[k, p], dev)

    def wland(k, p, dst):
        rc(dst, dst, wsend.at[k, p], wrecv.at[k, p], dC).wait_recv()

    pair = z // 2

    def c_as(p):
        rows = pl.ds(pl.multiple_of((1 - pair) * 1024, 1024), 1024)
        return wcopy(AS, p, PA.at[p, rows], RSA.at[p], dS)

    def c_ap(p):
        return wcopy(AP, p, SPA.at[p], QA.at[p, :, role], dP)

    def c_ax1(p):
        return (
            wcopy(AX1P, p, QA.at[p, x2, 0], R1.at[p, 0], dXp),
            wcopy(AX1M, p, QA.at[p, x2, 1], R1.at[p, 1], dXm),
        )

    def c_ax2(p):
        return (
            wcopy(AX2P, p, QA.at[p, xp], R2.at[p, 0], dXp),
            wcopy(AX2M, p, QA.at[p, xm], R2.at[p, 1], dXm),
        )

    def c_bx1(p):
        return (
            wcopy(BX1P, p, PB.at[p, x2, pl.ds(0, 2)], T1.at[p, 0], dXp),
            wcopy(BX1M, p, PB.at[p, x2, pl.ds(2, 2)], T1.at[p, 1], dXm),
        )

    def c_bx2(p):
        return (
            wcopy(BX2P, p, PB.at[p, xp], T2.at[p, 0], dXp),
            wcopy(BX2M, p, PB.at[p, xm], T2.at[p, 1], dXm),
        )

    def c_bs(p):
        return wcopy(BSK, p, BS.at[p], U1.at[p], dS)

    def c_bp(p):
        return wcopy(BPK, p, BP.at[p], U2.at[p], dP)

    def weights(lo, hi):
        @pl.loop(lo, hi)
        def _(p):
            mi, j = p // 2, p % 2

            @pl.loop(0, 4)
            def _(rb):
                rows = pl.ds(pl.multiple_of(rb * HALF, HALF), HALF)
                res = jnp.dot(
                    LT[mi // 2, rows, :],
                    G[mi, :, pl.ds(pl.multiple_of(j * 256, 256), 256)],
                    preferred_element_type=F32,
                ).astype(BF16)
                PA[p, rows, :] = res[:, :128]
                for xd in range(4):
                    PB[p, xd, rb] = res[xd * 128 : (xd + 1) * 128, 128:]

            c_as(p).start()
            for d in c_bx1(p):
                d.start()

    def plus(a, b):
        return a.astype(F32) + b.astype(F32)

    def step_bx2(lo, hi):
        @pl.loop(lo, hi)
        def _(p):
            up, down = c_bx2(p)
            wland(BX1P, p, T1.at[p, 0])
            for i in range(2):
                PB[p, xp, i] = plus(PB[p, xp, i], T1[p, 0, i]).astype(BF16)
            up.start()
            wland(BX1M, p, T1.at[p, 1])
            for i in range(2):
                PB[p, xm, 2 + i] = plus(PB[p, xm, 2 + i], T1[p, 1, i]).astype(BF16)
            down.start()

    def step_bs(lo, hi):
        @pl.loop(lo, hi)
        def _(p):
            wland(BX2P, p, T2.at[p, 0])
            wland(BX2M, p, T2.at[p, 1])
            for i in range(2):
                o = 2 * (1 - pair) + i
                BS[p, i] = (plus(PB[p, x, o], T2[p, 0, o]) + T2[p, 1, o].astype(F32)).astype(BF16)
            c_bs(p).start()
            for i in range(2):
                o = 2 * pair + i
                BK[p, i] = plus(PB[p, x, o], T2[p, 0, o]) + T2[p, 1, o].astype(F32)

    def out_cols(p, half, off):
        return pl.ds(pl.multiple_of(half * HALF + (p % 2) * 256 + off, 128), 128)

    def step_bp(lo, hi):
        @pl.loop(lo, hi)
        def _(p):
            wland(BSK, p, U1.at[p])
            BP[p] = plus(BK[p, zp % 2], U1[p, zp % 2]).astype(BF16)
            c_bp(p).start()
            gr_ref[p // 2, :, out_cols(p, role, 128)] = plus(BK[p, z % 2], U1[p, z % 2])

    def step_bf(lo, hi):
        @pl.loop(lo, hi)
        def _(p):
            wland(BPK, p, U2.at[p])
            gr_ref[p // 2, :, out_cols(p, 1 - role, 128)] = U2[p].astype(F32)

    def step_ap(lo, hi):
        @pl.loop(lo, hi)
        def _(p):
            wland(AS, p, RSA.at[p])
            for xd in range(4):
                ra = pl.ds(pl.multiple_of(zp * HALF + xd * 128, 128), 128)
                rr = pl.ds(pl.multiple_of((zp % 2) * HALF + xd * 128, 128), 128)
                SPA[p, xd] = plus(PA[p, ra, :], RSA[p, rr, :]).astype(BF16)
            c_ap(p).start()
            for xd in range(4):
                ra = pl.ds(pl.multiple_of(z * HALF + xd * 128, 128), 128)
                rr = pl.ds(pl.multiple_of((z % 2) * HALF + xd * 128, 128), 128)
                QA[p, xd, role] = plus(PA[p, ra, :], RSA[p, rr, :]).astype(BF16)

    def step_ax1(lo, hi):
        @pl.loop(lo, hi)
        def _(p):
            wland(AP, p, QA.at[p, :, 1 - role])
            for d in c_ax1(p):
                d.start()

    def step_ax2(lo, hi):
        @pl.loop(lo, hi)
        def _(p):
            up, down = c_ax2(p)
            wland(AX1P, p, R1.at[p, 0])
            QA[p, xp, 0] = plus(QA[p, xp, 0], R1[p, 0]).astype(BF16)
            up.start()
            wland(AX1M, p, R1.at[p, 1])
            QA[p, xm, 1] = plus(QA[p, xm, 1], R1[p, 1]).astype(BF16)
            down.start()

    def step_af(lo, hi):
        @pl.loop(lo, hi)
        def _(p):
            wland(AX2P, p, R2.at[p, 0])
            wland(AX2M, p, R2.at[p, 1])
            for h in range(2):
                gr_ref[p // 2, :, out_cols(p, h, 0)] = plus(QA[p, x, h], R2[p, 0, h]) + R2[
                    p, 1, h
                ].astype(F32)

    def ycopy(e, k):
        lo, hi = pl.ds(0, ROWS), pl.ds(ROWS, ROWS)
        a, b, d = (
            (ES.at[e], ER.at[e], dC),
            (EK.at[e, y2, lo], V1.at[e, 0], dYp),
            (EK.at[e, y2, hi], V1.at[e, 1], dYm),
            (EK.at[e, yp], V2.at[e, 0], dYp),
            (EK.at[e, ym], V2.at[e, 1], dYm),
            (WS.at[e], W1.at[e], dP),
        )[k]
        return rc(a, b, ysend.at[e, k], yrecv.at[e, k], d)

    def yland(e, k):
        b = (ER.at[e], V1.at[e, 0], V1.at[e, 1], V2.at[e, 0], V2.at[e, 1], W1.at[e])[k]
        rc(b, b, ysend.at[e, k], yrecv.at[e, k], dC).wait_recv()

    def nt(a, b):
        return lax.dot_general(a, b, (((1,), (1,)), ((), ())), preferred_element_type=F32)

    def y_compute(e):
        def block(dst, cc):
            @pl.loop(0, 4)
            def _(yy):
                rows = pl.ds(pl.multiple_of((yy * 2 + cc) * FEAT, FEAT), FEAT)
                if e == 0:
                    v = nt(G[0], W[0, rows, :]) + nt(G[1], W[1, rows, :])
                else:
                    v = nt(G[2], W[2, rows, :])
                dst[e, yy] = v.astype(BF16)

        block(ES, 1 - c)
        ycopy(e, 0).start()
        block(EK, c)

    def y_v1(e):
        yland(e, 0)
        for yy in (y2, yp, ym, y):
            @pl.loop(0, 6)
            def _(i):
                r = pl.ds(pl.multiple_of(i * 128, 128), 128)
                EK[e, yy, r, :] = plus(EK[e, yy, r, :], ER[e, yy, r, :]).astype(BF16)

            if yy is y2:
                ycopy(e, 1).start()
                ycopy(e, 2).start()

    def y_v2(e):
        for d, (k, yy) in enumerate(((1, yp), (2, ym))):
            yland(e, k)

            @pl.loop(0, 3)
            def _(i):
                r = pl.ds(pl.multiple_of(d * ROWS + i * 128, 128), 128)
                rv = pl.ds(pl.multiple_of(i * 128, 128), 128)
                EK[e, yy, r, :] = plus(EK[e, yy, r, :], V1[e, d, rv, :]).astype(BF16)

            ycopy(e, k + 2).start()

    def y_p(e):
        yland(e, 3)
        yland(e, 4)

        @pl.loop(0, 3)
        def _(i):
            r = pl.ds(pl.multiple_of(ROWS + i * 128, 128), 128)
            rv = pl.ds(pl.multiple_of(i * 128, 128), 128)
            WS[e, rv, :] = (
                plus(EK[e, y, r, :], V2[e, 0, r, :]) + V2[e, 1, r, :].astype(F32)
            ).astype(BF16)

        ycopy(e, 5).start()

        @pl.loop(0, 3)
        def _(i):
            r = pl.ds(pl.multiple_of(i * 128, 128), 128)
            FS[e, r, :] = plus(EK[e, y, r, :], V2[e, 0, r, :]) + V2[e, 1, r, :].astype(F32)

    def y_block_out():
        yland(1, 5)
        for b in range(NB):
            rows = slice(b * BLK, (b + 1) * BLK)
            branch = FS[1, rows, :] + W1[1, rows, :].astype(F32)
            bo_ref[rows, :] = (XT[rows, :].astype(F32) + branch).astype(BF16)

    def y_partial():
        yland(0, 5)
        for b in range(NB):
            rows = slice(b * BLK, (b + 1) * BLK)
            g = FS[0, rows, :] + W1[0, rows, :].astype(F32)
            FS[0, rows, :] = g
            BSUM[b : b + 1, :] = jnp.sum(g * NRM[rows, :], axis=0, keepdims=True)
        PS[t] = jnp.dot(
            onehot, BSUM[...], precision=HIGHEST, preferred_element_type=F32
        ).astype(BF16)
        table_send(PS, 1)

    def y_grad_tokens():
        total = table_sum(PS, 1)
        gg_ref[...] = jnp.sum(total, axis=0, keepdims=True)
        BSUM[...] = jnp.dot(
            onehot_t, gain * total / GHOST, precision=HIGHEST, preferred_element_type=F32
        )
        for b in range(NB):
            rows = slice(b * BLK, (b + 1) * BLK)
            g, nb = FS[0, rows, :], NRM[rows, :]
            dyb = DYB[0, rows, own_cols].astype(F32)
            gt_ref[rows, :] = (
                dyb + SCB[b : b + 1, :] * (gain * g - nb * BSUM[b : b + 1, :])
            ).astype(BF16)

    weights(0, 3)
    y_compute(0)
    weights(3, 6)
    y_v1(0)
    step_ap(0, 1)
    y_compute(1)
    step_bx2(0, 3)
    step_ax1(0, 1)
    step_ap(1, 2)
    y_v1(1)
    step_bx2(3, 6)
    y_v2(0)
    step_ax2(0, 1)
    step_ax1(1, 2)
    step_bs(0, 2)
    step_ap(2, 3)
    y_v2(1)
    step_ax2(1, 2)
    step_ax1(2, 3)
    step_bs(2, 4)
    step_ap(3, 4)
    y_p(0)
    step_ax2(2, 3)
    step_bs(4, 6)
    step_ax1(3, 4)
    y_partial()
    step_ap(4, 5)
    step_ax2(3, 4)
    y_p(1)
    step_ax1(4, 5)
    step_ap(5, 6)
    step_ax2(4, 5)
    step_ax1(5, 6)
    y_grad_tokens()
    y_block_out()
    step_af(0, 4)
    step_bp(0, 2)
    step_ax2(5, 6)
    step_bp(2, 6)
    step_af(4, 6)
    step_bf(0, 6)

    for g, B in ((0, DYB), (1, HB)):
        for k in range(16):
            gcopy(B, g, k).wait_send()
    for e, buf in ((0, SB), (1, PS)):
        for k in range(1, TOK):
            rc(buf.at[t], buf.at[t], ssend.at[e, k], srecv.at[e, k], dC).wait_send()
    for e in range(2):
        for k in range(6):
            ycopy(e, k).wait_send()

    @pl.loop(0, PIECES)
    def _(p):
        for d in (
            c_as(p), c_ap(p), *c_ax1(p), *c_ax2(p), *c_bx1(p), *c_bx2(p), c_bs(p), c_bp(p)
        ):
            d.wait_send()


def body(tokens, norm_gain, running_sq, gate_weight, up_weight, down_weight_t, groups, cotangent):
    V = pltpu.VMEM
    any_spec = pl.BlockSpec(memory_space=pl.ANY)
    vmem_spec = pl.BlockSpec(memory_space=pltpu.VMEM)
    n = PIECES
    sq = (128, 128)
    dma = pltpu.SemaphoreType.DMA
    scratch = [
        V((ROWS, FEAT), BF16), V((ROWS, FEAT), F32), V((NB, FEAT), F32), V((NB, FEAT), F32),
        V((2, ROWS, WIDTH), BF16), V((2, ROWS, WIDTH), BF16), V((2, WIDTH, 2 * ROWS), BF16),
        V((3, WIDTH, HALF), BF16), V((3, 2 * ROWS, HALF), BF16),
        V((ROWS, HALF), F32), V((ROWS, HALF), F32), V((2, ROWS, HALF), F32),
        V((TOK, GROUPS, FEAT), BF16), V((TOK, GROUPS, FEAT), BF16),
        V((n, WIDTH, 128), BF16), V((n, 1024, 128), BF16), V((n, 4, *sq), BF16),
        V((n, 4, 2, *sq), BF16), V((n, 2, *sq), BF16), V((n, 2, 2, *sq), BF16),
        V((n, 4, 4, *sq), BF16), V((n, 2, 2, *sq), BF16), V((n, 2, 4, *sq), BF16),
        V((n, 2, *sq), F32), V((n, 2, *sq), BF16), V((n, 2, *sq), BF16),
        V((n, *sq), BF16), V((n, *sq), BF16),
        V((2, 4, 2 * ROWS, FEAT), BF16), V((2, 4, 2 * ROWS, FEAT), BF16),
        V((2, 4, 2 * ROWS, FEAT), BF16), V((2, 2, ROWS, FEAT), BF16),
        V((2, 2, 2 * ROWS, FEAT), BF16), V((2, ROWS, FEAT), BF16), V((2, ROWS, FEAT), BF16),
        V((2, ROWS, FEAT), F32),
        dma((5,)), dma((2, 16)), dma((2, 16)), dma((2, TOK)), dma((2, TOK)),
        dma((12, n)), dma((12, n)), dma((2, 6)), dma((2, 6)),
    ]
    block_out, grad_tokens, run_new, gain_grad, grads = pl.pallas_call(
        kernel,
        out_shape=(
            jax.ShapeDtypeStruct((ROWS, FEAT), BF16),
            jax.ShapeDtypeStruct((ROWS, FEAT), BF16),
            jax.ShapeDtypeStruct((1, FEAT), F32),
            jax.ShapeDtypeStruct((1, FEAT), F32),
            jax.ShapeDtypeStruct((3, 128, 1024), F32),
        ),
        in_specs=[any_spec, vmem_spec, vmem_spec, any_spec, any_spec, any_spec, vmem_spec, any_spec],
        out_specs=(vmem_spec,) * 5,
        scratch_shapes=scratch,
        compiler_params=pltpu.CompilerParams(
            collective_id=0, has_side_effects=True, vmem_limit_bytes=67043328
        ),
    )(
        tokens, norm_gain.reshape(1, -1), running_sq.reshape(1, -1), gate_weight, up_weight,
        down_weight_t, groups.reshape(1, -1), cotangent,
    )
    return (
        block_out, grad_tokens, run_new.reshape(-1), gain_grad.reshape(-1),
        grads[0], grads[1], grads[2],
    )


def solution(mesh):
    placed = (
        P("tok", "mp"),
        P(),
        P("mp"),
        P(None, "mp"),
        P(None, "mp"),
        P(None, "mp"),
        P("tok"),
        P("tok", "mp"),
    )
    return jax.shard_map(
        body,
        mesh=mesh,
        in_specs=placed,
        out_specs=(
            P("tok", "mp"),
            P("tok", "mp"),
            P("mp"),
            P("mp"),
            P("tok", "mp"),
            P("tok", "mp"),
            P("tok", "mp"),
        ),
        check_vma=False,
    )
```

time: 234 us -> 132 us (0.56)
  Pallas kernels: 0 us -> 122 us
  waiting for transfers between devices: 105 us -> 0 us
  matrix products: 32.8 us -> 0 us
  starting transfers between devices: 29.9 us -> 0 us
  local copies, waits for them, and re-layouts: 31 us -> 8.21 us
  other arithmetic: 18.2 us -> 0 us
  between operations: 14.4 us -> 0.65 us
    pallas_call x0 -> x1, Pallas kernels: none -> 122 us  [body(): pl.pallas_call(kernel, out_shape=(jax.ShapeDtypeStruct((ROWS, FEAT), BF16...]
    all_to_all x6 -> x0, waiting for transfers between devices: 89 us -> none  [the longest x4 52.6 us: from_everyone(): return lax.all_to_all(copies, axis, split_axis=0, concat_axis=0, tiled=True)]
    dot_general x12 -> x0, matrix products: 32.8 us -> none  [the longest x3 10.1 us: contract_cols(): lax.dot_general(left, right, (((1,), (1,)), ((), ())), preferred_element_...]
    all_to_all x6 -> x0, starting transfers between devices: 29.9 us -> none  [the longest x4 22.4 us: from_everyone(): return lax.all_to_all(copies, axis, split_axis=0, concat_axis=0, tiled=True)]
    unnamed x46 -> x4, local copies, waits for them, and re-layouts: 23.2 us -> 5.66 us
    unnamed x2 -> x0, waiting for transfers between devices: 16.3 us -> none
    concatenate x1 -> x0, other arithmetic: 14.4 us -> none  [body(): jnp.concatenate([upper, lower], axis=1).astype(jnp.bfloat16)]
    broadcast_in_dim x4 -> x0, local copies, waits for them, and re-layouts: 4.33 us -> none  [from_everyone(): copies = jnp.broadcast_to(x, (lax.axis_size(axis), *x.shape))]
  transfers between devices with their start and end apart: 7 -> 0, of which waited for: 7 -> 0; matrix products, arithmetic and copies ran while one was open for 11% -> 0% of each run, Pallas kernels for 0% -> 0%
where the time goes in v1:
time: 132 us; the launch traced here: 131 us
  Pallas kernels  122 us (92%)
  local copies, waits for them, and re-layouts  8.21 us (6%)
    pallas_call x1, Pallas kernels, body(): pl.pallas_call(kernel, out_shape=(jax.ShapeDtypeStruct((ROWS, FEAT), BF16...  122 us
    unnamed x4, local copies, waits for them, and re-layouts  5.66 us

profile of v1, /device:TPU:32, one launch (start us, length us, event | category | flops | bytes accessed | tf_op | source)
XLA Modules:
  0.0 131.3 jit_solution(4959224557097941166)
XLA Ops:
  0.6 122.5 %shard_map.135 = (bf16[384,256]{1,0:T(8,128)(2,1)}, bf16[384,256]{1,0:T(8,128)(2,1)}, f32[1,256]{1,0:T(1,128)}, f32[1,256]{1,0:T(1,128)}, f32[3,128,1024]{2,1,0:T(8,128)}) custom-call(bf16[384,256]{1,0:T(8,128)(2,1)} %tok_hbm.1, f32[1,2048]{1,0:T(1,128)} %bitcast.11, f32[1,256]{1,0:T(1,128)} %bitcast.12, bf16[2048,1024]{1,0:T(8,128)(2,1)} %gw_hbm.1, ...), custom_call_target="tpu_custom_call" | custom-call | tf_op jit(solution)/shard_map/pallas_call | solution.py:616
  123.1 2.5 %slice_bitcast_fusion = (f32[128,1024]{1,0:T(8,128)}, f32[128,1024]{1,0:T(8,128)}, f32[128,1024]{1,0:T(8,128)}) fusion(f32[3,128,1024]{2,1,0:T(8,128)} %get-tuple-element.16), kind=kLoop, calls=%fused_computation | loop fusion | bytes 3145728 | tf_op jit(solution)/shard_map/squeeze | solution.py:637
  125.7 1.6 %copy.19 = bf16[384,256]{1,0:T(8,128)(2,1)} copy(bf16[384,256]{1,0:T(8,128)(2,1)} %get-tuple-element.27) | data formatting | bytes 393216
  127.3 1.6 %copy.20 = bf16[384,256]{1,0:T(8,128)(2,1)} copy(bf16[384,256]{1,0:T(8,128)(2,1)} %get-tuple-element.28) | data formatting | bytes 393216
  128.9 1.2 copy.21
  130.1 1.2 copy.22

commit v2 on v0

v2 whole, which is shorter than its diff:
```python
import jax
import jax.numpy as jnp
from jax import lax
from jax.experimental import pallas as pl
from jax.experimental.pallas import tpu as pltpu
from jax.sharding import PartitionSpec as P

GHOST = 128
BLK = 16
ROWS = 384
FEAT = 256
WIDTH = 2048
HALF = 512
GROUPS = 48
NB = 24
A_PARTS = tuple((p, 0) for p in range(5))
B_PARTS = tuple((p, 1) for p in range(5)) + ((5, 0), (5, 1))

epsilon = 1e-05
momentum = 0.1
F32 = jnp.float32
BF16 = jnp.bfloat16
HIGHEST = lax.Precision.HIGHEST


def kernel(
    tok_hbm, gain_ref, run_ref, gw_hbm, uw_hbm, dw_hbm, grp_ref, cot_hbm,
    bo_ref, gt_ref, rn_ref, gg_ref, gr_ref,
    XT, NRM, BSUM, SCB, DYB, HB, LT, W, G, GT, LF, GH,
    TZ, TX, PA, RSA, SPA, QA, R1, R2, PB, T1, T2, BK, BS, U1, BP, U2,
    EK, ES, ER, V1, V2, WS, W1, FS,
    lsem, gsend, grecv, ssend, srecv, asend, arecv, bsend, brecv, ysend, yrecv, csend, crecv,
):
    t = lax.axis_index("tok")
    m = lax.axis_index("mp")
    z, x = t // 4, t % 4
    y, c = m // 2, m % 2
    zp = z + 1 - 2 * (z % 2)
    zs = 3 - z
    role = ((z + 1) // 2) % 2
    yp, ym, y2 = (y + 1) % 4, (y + 3) % 4, (y + 2) % 4
    xp, xm, x2 = (x + 1) % 4, (x + 3) % 4, (x + 2) % 4
    dC = (t, y * 2 + 1 - c)
    dP = (zp * 4 + x, m)
    dS = (zs * 4 + x, m)
    dYp, dYm = (t, yp * 2 + c), (t, ym * 2 + c)
    dXp, dXm = (z * 4 + xp, m), (z * 4 + xm, m)

    def rc(src, dst, ss, rs, dev):
        return pltpu.make_async_remote_copy(
            src_ref=src, dst_ref=dst, send_sem=ss, recv_sem=rs,
            device_id=dev, device_id_type=pl.DeviceIdType.MESH,
        )

    own_cols = pl.ds(pl.multiple_of(m * FEAT, FEAT), FEAT)

    cp_dy = pltpu.make_async_copy(cot_hbm, DYB.at[0, :, own_cols], lsem.at[0])
    cp_dy.start()
    cp_x = pltpu.make_async_copy(tok_hbm, XT, lsem.at[1])
    cp_x.start()
    wcols = pl.ds(pl.multiple_of(role * HALF, HALF), HALF)
    cp_w = [
        pltpu.make_async_copy(h.at[:, wcols], W.at[i], lsem.at[2 + i])
        for i, h in enumerate((gw_hbm, uw_hbm, dw_hbm))
    ]
    for k in (2, 0, 1):
        cp_w[k].start()

    bar = pltpu.get_barrier_semaphore()
    z_others = [(((z + k) % 4) * 4 + x, m) for k in range(1, 4)]
    x_others = [(z * 4 + (x + k) % 4, m) for k in range(1, 4)]
    for d in (*z_others, *x_others, dC, dYp, dYm):
        pl.semaphore_signal(bar, inc=1, device_id=d, device_id_type=pl.DeviceIdType.MESH)

    def sl(B, slot, yy, cc, r0=0, n=ROWS):
        return B.at[slot, pl.ds(r0, n), pl.ds(pl.multiple_of((yy * 2 + cc) * FEAT, FEAT), FEAT)]

    def gcopy(B, g, k):
        h = ROWS // 2
        if k == 0:
            a, b, d = sl(B, 0, y, c), sl(B, 1, y, c), dP
        elif k in (1, 16):
            a = b = sl(B, 0, y, c, 0 if k == 1 else h, h)
            d = dYp
        elif k in (2, 17):
            a = b = sl(B, 0, y, c, h if k == 2 else 0, h)
            d = dYm
        elif k == 3:
            a = b = sl(B, 0, ym, c, 0, h)
            d = dYp
        elif k == 4:
            a = b = sl(B, 0, yp, c, h, h)
            d = dYm
        elif k == 5:
            a = b = sl(B, 1, y, c)
            d = dYp
        elif k == 6:
            a = b = sl(B, 1, y, c)
            d = dYm
        elif k == 7:
            a, b, d = sl(B, 0, y2, c), sl(B, 1, y2, c), dP
        else:
            slot = (k - 8) // 4
            yy = (y, ym, yp, y2)[(k - 8) % 4]
            a = b = sl(B, slot, yy, c)
            d = dC
        return rc(a, b, gsend.at[g, k], grecv.at[g, k], d)

    def gland(B, g, k):
        h = ROWS // 2
        if k == 0:
            b = sl(B, 1, y, c)
        elif k in (1, 16):
            b = sl(B, 0, ym, c, 0 if k == 1 else h, h)
        elif k in (2, 17):
            b = sl(B, 0, yp, c, h if k == 2 else 0, h)
        elif k == 3:
            b = sl(B, 0, y2, c, 0, h)
        elif k == 4:
            b = sl(B, 0, y2, c, h, h)
        elif k == 5:
            b = sl(B, 1, ym, c)
        elif k == 6:
            b = sl(B, 1, yp, c)
        elif k == 7:
            b = sl(B, 1, y2, c)
        else:
            b = sl(B, (k - 8) // 4, (y, ym, yp, y2)[(k - 8) % 4], 1 - c)
        rc(b, b, gsend.at[g, k], grecv.at[g, k], dC).wait_recv()

    def gstart(B, g, *ks):
        for k in ks:
            gcopy(B, g, k).start()

    def send_own(B, g):
        gstart(B, g, 1, 2, 0, 16, 17, 8)

    def fwd(B, g, land, *sends):
        for k in land:
            gland(B, g, k)
        gstart(B, g, *sends)

    def tcopy(e, a, k):
        buf, me, d = ((TZ, z, z_others), (TX, x, x_others))[a]
        ref = buf.at[e, me]
        return rc(ref, ref, ssend.at[e, a, k], srecv.at[e, a, k], d[k - 1])

    def tsum(e, a):
        buf, me = ((TZ, z), (TX, x))[a]
        for k in range(1, 4):
            ref = buf.at[e, (me + 4 - k) % 4]
            rc(ref, ref, ssend.at[e, a, k], srecv.at[e, a, k], dC).wait_recv()
        return (buf[e, 0].astype(F32) + buf[e, 1].astype(F32)) + (
            buf[e, 2].astype(F32) + buf[e, 3].astype(F32)
        )

    def tsend(e, a):
        for k in range(1, 4):
            tcopy(e, a, k).start()

    def tmid(e):
        TX[e, x] = tsum(e, 0).astype(BF16)
        tsend(e, 1)

    grow = grp_ref[...]
    onehot = (
        lax.broadcasted_iota(jnp.int32, (GROUPS, NB), 0) == jnp.broadcast_to(grow, (GROUPS, NB))
    ).astype(F32)
    diag = lax.broadcasted_iota(jnp.int32, (NB, NB), 0) == lax.broadcasted_iota(
        jnp.int32, (NB, NB), 1
    )
    gcol = jnp.sum(
        jnp.where(diag, jnp.broadcast_to(grow, (NB, NB)), 0).astype(F32), axis=1, keepdims=True
    )
    onehot_t = (
        lax.broadcasted_iota(jnp.int32, (NB, GROUPS), 1).astype(F32)
        == jnp.broadcast_to(gcol, (NB, GROUPS))
    ).astype(F32)

    gain = gain_ref[:, own_cols]

    def start():
        cp_x.wait()
        for b in range(NB):
            xb = XT[b * BLK : (b + 1) * BLK, :].astype(F32)
            BSUM[b : b + 1, :] = jnp.sum(xb * xb, axis=0, keepdims=True)
        TZ[0, z] = jnp.dot(
            onehot, BSUM[...], precision=HIGHEST, preferred_element_type=F32
        ).astype(BF16)
        cp_dy.wait()
        pl.semaphore_wait(bar, 9)
        tsend(0, 0)
        send_own(DYB, 0)

    def stat2():
        quad = tsum(0, 1) / GHOST
        rn_ref[...] = (1.0 - momentum) * run_ref[...] + momentum * (
            jnp.sum(quad, axis=0, keepdims=True) / GROUPS
        )
        SCB[...] = jnp.dot(
            onehot_t, lax.rsqrt(quad + epsilon), precision=HIGHEST, preferred_element_type=F32
        )
        for b in range(NB):
            rows = slice(b * BLK, (b + 1) * BLK)
            nb = XT[rows, :].astype(F32) * SCB[b : b + 1, :]
            NRM[rows, :] = nb
            HB[0, rows, own_cols] = (gain * nb).astype(BF16)

    def transposed(B, i, slot):
        @pl.loop(0, 8)
        def _(j):
            cols = pl.ds(pl.multiple_of(j * FEAT, FEAT), FEAT)
            LT[i, cols, pl.ds(slot * ROWS, ROWS)] = B[slot, :, cols].T

    def units(slot):
        if slot == 0:
            cp_w[0].wait()
            cp_w[1].wait()
        GT[...] = jnp.dot(HB[slot], W[0], preferred_element_type=F32)
        LF[...] = jnp.dot(HB[slot], W[1], preferred_element_type=F32)

        @pl.loop(0, ROWS // 16)
        def _(i):
            r = pl.ds(pl.multiple_of(i * 16, 16), 16)
            ro = pl.ds(pl.multiple_of(slot * ROWS + i * 16, 16), 16)
            gate, lift, gh = GT[r, :], LF[r, :], GH[slot, r, :]
            sigma = jax.nn.sigmoid(gate)
            G[0, ro, :] = (gate * sigma * lift).astype(BF16)
            G[1, ro, :] = (gh * lift * sigma * (1.0 + gate * (1.0 - sigma))).astype(BF16)
            G[2, ro, :] = (gh * gate * sigma).astype(BF16)

    def gh(slot):
        if slot == 0:
            cp_w[2].wait()
        GH[slot] = jnp.dot(DYB[slot], W[2], preferred_element_type=F32)

    def slot_ready(B, g, slot):
        for k in range(8 + 4 * slot, 12 + 4 * slot):
            gland(B, g, k)

    AS, AP, AX1P, AX1M, AXIP, AXIM, AX2P, AX2M = range(8)
    BX1P, BX1M, BXIP, BXIM, BX2P, BX2M, BSK, BPK = range(8)
    pair = z // 2
    lo2, hi2 = pl.ds(0, 2), pl.ds(2, 2)

    def a_copy(k, a):
        far = pl.ds(pl.multiple_of((1 - pair) * 1024, 1024), 1024)
        src, dst, d = (
            (PA.at[a, far], RSA.at[a], dS),
            (SPA.at[a], QA.at[a, :, role], dP),
            (QA.at[a, x2, 0], R1.at[a, 0], dXp),
            (QA.at[a, x2, 1], R1.at[a, 1], dXm),
            (QA.at[a, xp, 1], R2.at[a, 0, 1], dXp),
            (QA.at[a, xm, 0], R2.at[a, 1, 0], dXm),
            (QA.at[a, xp, 0], R2.at[a, 0, 0], dXp),
            (QA.at[a, xm, 1], R2.at[a, 1, 1], dXm),
        )[k]
        return rc(src, dst, asend.at[k, a], arecv.at[k, a], d)

    def a_land(k, a):
        b = (
            RSA.at[a], QA.at[a, :, 1 - role], R1.at[a, 0], R1.at[a, 1],
            R2.at[a, 0, 1], R2.at[a, 1, 0], R2.at[a, 0, 0], R2.at[a, 1, 1],
        )[k]
        rc(b, b, asend.at[k, a], arecv.at[k, a], dC).wait_recv()

    def b_copy(k, b):
        src, dst, d = (
            (PB.at[b, x2, lo2], T1.at[b, 0], dXp),
            (PB.at[b, x2, hi2], T1.at[b, 1], dXm),
            (PB.at[b, xp, hi2], T2.at[b, 0, hi2], dXp),
            (PB.at[b, xm, lo2], T2.at[b, 1, lo2], dXm),
            (PB.at[b, xp, lo2], T2.at[b, 0, lo2], dXp),
            (PB.at[b, xm, hi2], T2.at[b, 1, hi2], dXm),
            (BS.at[b], U1.at[b], dS),
            (BP.at[b], U2.at[b], dP),
        )[k]
        return rc(src, dst, bsend.at[k, b], brecv.at[k, b], d)

    def b_land(k, b):
        r = (
            T1.at[b, 0], T1.at[b, 1], T2.at[b, 0, hi2], T2.at[b, 1, lo2],
            T2.at[b, 0, lo2], T2.at[b, 1, hi2], U1.at[b], U2.at[b],
        )[k]
        rc(r, r, bsend.at[k, b], brecv.at[k, b], dC).wait_recv()

    def weights(p):
        mi, j = p // 2, p % 2

        @pl.loop(0, 2)
        def _(rh):
            rows = pl.ds(pl.multiple_of(rh * 1024, 1024), 1024)
            res = jnp.dot(
                LT[(mi + 1) // 2, rows, :],
                G[mi, :, j * 256 : (j + 1) * 256],
                preferred_element_type=F32,
            ).astype(BF16)
            for off in range(2):
                part = res[:, off * 128 : (off + 1) * 128]
                if (p, off) in A_PARTS:
                    PA[A_PARTS.index((p, off)), rows, :] = part
                else:
                    b = B_PARTS.index((p, off))
                    for i in range(8):
                        PB[b, i % 4, rh * 2 + i // 4] = part[i * 128 : (i + 1) * 128]

        for off in range(2):
            if (p, off) in A_PARTS:
                a_copy(AS, A_PARTS.index((p, off))).start()
        for ks in ((BX1P, BX1M), (BXIP, BXIM)):
            for off in range(2):
                if (p, off) in B_PARTS:
                    for k in ks:
                        b_copy(k, B_PARTS.index((p, off))).start()

    def plus(a, b):
        return a.astype(F32) + b.astype(F32)

    def out_cols(part, half):
        p, off = part
        return pl.ds(pl.multiple_of(half * HALF + (p % 2) * 256 + off * 128, 128), 128)

    def step_ap(a):
        a_land(AS, a)
        for xd in range(4):
            ra = pl.ds(pl.multiple_of(zp * HALF + xd * 128, 128), 128)
            rr = pl.ds(pl.multiple_of((zp % 2) * HALF + xd * 128, 128), 128)
            SPA[a, xd] = plus(PA[a, ra, :], RSA[a, rr, :]).astype(BF16)
        a_copy(AP, a).start()
        for xd in range(4):
            ra = pl.ds(pl.multiple_of(z * HALF + xd * 128, 128), 128)
            rr = pl.ds(pl.multiple_of((z % 2) * HALF + xd * 128, 128), 128)
            QA[a, xd, role] = plus(PA[a, ra, :], RSA[a, rr, :]).astype(BF16)

    def step_ax1(a):
        a_land(AP, a)
        for k in (AX1P, AX1M, AXIP, AXIM):
            a_copy(k, a).start()

    def step_ax2(a):
        a_land(AX1P, a)
        QA[a, xp, 0] = plus(QA[a, xp, 0], R1[a, 0]).astype(BF16)
        a_copy(AX2P, a).start()
        a_land(AX1M, a)
        QA[a, xm, 1] = plus(QA[a, xm, 1], R1[a, 1]).astype(BF16)
        a_copy(AX2M, a).start()

    def step_af(a):
        for k in (AXIP, AXIM, AX2P, AX2M):
            a_land(k, a)
        for h in range(2):
            gr_ref[A_PARTS[a][0] // 2, :, out_cols(A_PARTS[a], h)] = plus(
                QA[a, x, h], R2[a, 0, h]
            ) + R2[a, 1, h].astype(F32)

    def step_bx2(b):
        b_land(BX1P, b)
        for i in range(2):
            PB[b, xp, i] = plus(PB[b, xp, i], T1[b, 0, i]).astype(BF16)
        b_copy(BX2P, b).start()
        b_land(BX1M, b)
        for i in range(2):
            PB[b, xm, 2 + i] = plus(PB[b, xm, 2 + i], T1[b, 1, i]).astype(BF16)
        b_copy(BX2M, b).start()

    def step_bs(b):
        for k in (BXIP, BXIM, BX2P, BX2M):
            b_land(k, b)
        for i in range(2):
            o = 2 * (1 - pair) + i
            BS[b, i] = (plus(PB[b, x, o], T2[b, 0, o]) + T2[b, 1, o].astype(F32)).astype(BF16)
        b_copy(BSK, b).start()
        for i in range(2):
            o = 2 * pair + i
            BK[b, i] = plus(PB[b, x, o], T2[b, 0, o]) + T2[b, 1, o].astype(F32)

    def step_bp(b):
        b_land(BSK, b)
        BP[b] = plus(BK[b, zp % 2], U1[b, zp % 2]).astype(BF16)
        b_copy(BPK, b).start()
        gr_ref[B_PARTS[b][0] // 2, :, out_cols(B_PARTS[b], role)] = plus(
            BK[b, z % 2], U1[b, z % 2]
        )

    def step_bf(b):
        b_land(BPK, b)
        gr_ref[B_PARTS[b][0] // 2, :, out_cols(B_PARTS[b], 1 - role)] = U2[b].astype(F32)

    V1P, V1M, VIP, VIM, V2P, V2M, WSK = range(7)
    lo, hi = pl.ds(0, ROWS), pl.ds(ROWS, ROWS)
    y_of = (y2, yp, ym, y)

    def y_copy(k, e):
        a, b, d = (
            (EK.at[e, y2, lo], V1.at[e, 0], dYp),
            (EK.at[e, y2, hi], V1.at[e, 1], dYm),
            (EK.at[e, yp, hi], V2.at[e, 0, hi], dYp),
            (EK.at[e, ym, lo], V2.at[e, 1, lo], dYm),
            (EK.at[e, yp, lo], V2.at[e, 0, lo], dYp),
            (EK.at[e, ym, hi], V2.at[e, 1, hi], dYm),
            (WS.at[e], W1.at[e], dP),
        )[k]
        return rc(a, b, ysend.at[e, k], yrecv.at[e, k], d)

    def y_land(k, e):
        b = (
            V1.at[e, 0], V1.at[e, 1], V2.at[e, 0, hi], V2.at[e, 1, lo],
            V2.at[e, 0, lo], V2.at[e, 1, hi], W1.at[e],
        )[k]
        rc(b, b, ysend.at[e, k], yrecv.at[e, k], dC).wait_recv()

    def sib_copy(e, i):
        return rc(
            ES.at[e, y_of[i]], ER.at[e, y_of[i]], csend.at[e, i], crecv.at[e, i], dC
        )

    def nt(a, b):
        return lax.dot_general(a, b, (((1,), (1,)), ((), ())), preferred_element_type=F32)

    def y_product(e, yy, cc):
        rows = pl.ds(pl.multiple_of((yy * 2 + cc) * FEAT, FEAT), FEAT)
        if e == 0:
            v = nt(G[1], W[0, rows, :]) + nt(G[2], W[1, rows, :])
        else:
            v = nt(G[0], W[2, rows, :])
        return v.astype(BF16)

    def y_sib(e, i):
        ES[e, y_of[i]] = y_product(e, y_of[i], 1 - c)
        sib_copy(e, i).start()

    def y_own(e, i):
        EK[e, y_of[i]] = y_product(e, y_of[i], c)

    def y_merge(e, i, *sends):
        sib_copy(e, i).wait_recv()
        yy = y_of[i]

        @pl.loop(0, 6)
        def _(n):
            r = pl.ds(pl.multiple_of(n * 128, 128), 128)
            EK[e, yy, r, :] = plus(EK[e, yy, r, :], ER[e, yy, r, :]).astype(BF16)

        for k in sends:
            y_copy(k, e).start()

    def y_relay(e, d):
        y_land((V1P, V1M)[d], e)
        yy = (yp, ym)[d]

        @pl.loop(0, 3)
        def _(n):
            r = pl.ds(pl.multiple_of(d * ROWS + n * 128, 128), 128)
            rv = pl.ds(pl.multiple_of(n * 128, 128), 128)
            EK[e, yy, r, :] = plus(EK[e, yy, r, :], V1[e, d, rv, :]).astype(BF16)

        y_copy((V2P, V2M)[d], e).start()

    def y_p(e):
        y_land(VIP, e)
        y_land(V2M, e)

        @pl.loop(0, 3)
        def _(n):
            r = pl.ds(pl.multiple_of(ROWS + n * 128, 128), 128)
            rv = pl.ds(pl.multiple_of(n * 128, 128), 128)
            WS[e, rv, :] = (
                plus(EK[e, y, r, :], V2[e, 0, r, :]) + V2[e, 1, r, :].astype(F32)
            ).astype(BF16)

        y_copy(WSK, e).start()

    def y_f(e):
        y_land(VIM, e)
        y_land(V2P, e)

        @pl.loop(0, 3)
        def _(n):
            r = pl.ds(pl.multiple_of(n * 128, 128), 128)
            FS[e, r, :] = plus(EK[e, y, r, :], V2[e, 0, r, :]) + V2[e, 1, r, :].astype(F32)

    def y_block_out():
        y_land(WSK, 1)
        for b in range(NB):
            rows = slice(b * BLK, (b + 1) * BLK)
            branch = FS[1, rows, :] + W1[1, rows, :].astype(F32)
            bo_ref[rows, :] = (XT[rows, :].astype(F32) + branch).astype(BF16)

    def y_partial():
        y_land(WSK, 0)
        for b in range(NB):
            rows = slice(b * BLK, (b + 1) * BLK)
            g = FS[0, rows, :] + W1[0, rows, :].astype(F32)
            FS[0, rows, :] = g
            BSUM[b : b + 1, :] = jnp.sum(g * NRM[rows, :], axis=0, keepdims=True)
        TZ[1, z] = jnp.dot(
            onehot, BSUM[...], precision=HIGHEST, preferred_element_type=F32
        ).astype(BF16)
        tsend(1, 0)

    def y_grad_tokens():
        total = tsum(1, 1)
        gg_ref[...] = jnp.sum(total, axis=0, keepdims=True)
        BSUM[...] = jnp.dot(
            onehot_t, gain * total / GHOST, precision=HIGHEST, preferred_element_type=F32
        )
        for b in range(NB):
            rows = slice(b * BLK, (b + 1) * BLK)
            g, nb = FS[0, rows, :], NRM[rows, :]
            dyb = DYB[0, rows, own_cols].astype(F32)
            gt_ref[rows, :] = (
                dyb + SCB[b : b + 1, :] * (gain * g - nb * BSUM[b : b + 1, :])
            ).astype(BF16)

    start()
    tmid(0)
    fwd(DYB, 0, (2,), 4)
    fwd(DYB, 0, (1,), 3)
    fwd(DYB, 0, (16,), 9)
    fwd(DYB, 0, (17,), 10)
    fwd(DYB, 0, (0,), 5, 6, 12)
    stat2()
    fwd(DYB, 0, (3, 4), 7, 11)
    send_own(HB, 1)
    slot_ready(DYB, 0, 0)
    gh(0)
    transposed(DYB, 0, 0)
    fwd(DYB, 0, (6,), 14)
    fwd(DYB, 0, (5,), 13)
    fwd(DYB, 0, (7,), 15)
    fwd(HB, 1, (1,), 3)
    fwd(HB, 1, (2,), 4)
    slot_ready(DYB, 0, 1)
    transposed(DYB, 0, 1)
    gh(1)
    fwd(HB, 1, (16,), 9)
    fwd(HB, 1, (17,), 10)
    fwd(HB, 1, (0,), 5, 6, 12)
    fwd(HB, 1, (3, 4), 7, 11)
    slot_ready(HB, 1, 0)
    units(0)
    transposed(HB, 1, 0)
    fwd(HB, 1, (6,), 14)
    fwd(HB, 1, (5,), 13)
    fwd(HB, 1, (7,), 15)
    slot_ready(HB, 1, 1)
    units(1)
    weights(0)
    y_sib(0, 0)
    y_sib(1, 3)
    y_sib(0, 2)
    y_sib(1, 1)
    weights(1)
    y_own(0, 0)
    y_merge(0, 0, V1P, V1M)
    y_sib(0, 1)
    y_own(0, 1)
    y_own(1, 3)
    transposed(HB, 1, 1)
    weights(5)
    y_merge(0, 1, VIP)
    weights(2)
    step_bx2(1)
    y_own(0, 3)
    y_sib(1, 0)
    y_own(1, 0)
    y_sib(1, 2)
    y_own(0, 2)
    y_merge(0, 2, VIM)
    y_relay(0, 1)
    step_bx2(5)
    y_relay(0, 0)
    step_ap(0)
    step_bx2(0)
    y_sib(0, 3)
    weights(4)
    y_merge(1, 0, V1P, V1M)
    step_bx2(6)
    y_own(1, 2)
    y_merge(1, 2, VIM)
    y_own(1, 1)
    y_merge(1, 1, VIP)
    y_merge(0, 3)
    y_merge(1, 3)
    step_ap(1)
    weights(3)
    step_ax1(0)
    step_bx2(2)
    step_ax1(1)
    step_bs(1)
    step_ap(2)
    step_bs(5)
    y_p(0)
    y_f(0)
    step_bs(0)
    y_relay(1, 0)
    step_bx2(4)
    step_ax1(2)
    step_ap(4)
    y_relay(1, 1)
    step_bs(6)
    step_bx2(3)
    y_partial()
    step_ax2(0)
    step_ap(3)
    step_ax1(4)
    step_bs(2)
    step_bp(1)
    step_ax2(1)
    step_bp(5)
    y_p(1)
    y_f(1)
    step_bs(4)
    step_bp(0)
    step_ax2(2)
    step_ax1(3)
    step_bf(1)
    step_bp(6)
    tmid(1)
    step_bf(5)
    step_bs(3)
    step_af(0)
    step_bp(2)
    step_ax2(4)
    step_bp(4)
    step_af(1)
    step_af(2)
    step_bp(3)
    y_block_out()
    step_ax2(3)
    step_bf(0)
    step_bf(6)
    step_bf(2)
    step_af(4)
    y_grad_tokens()
    step_bf(4)
    step_af(3)
    step_bf(3)
    for g, B in ((0, DYB), (1, HB)):
        for k in range(18):
            gcopy(B, g, k).wait_send()
    for e in range(2):
        for a in range(2):
            for k in range(1, 4):
                tcopy(e, a, k).wait_send()
        for i in range(4):
            sib_copy(e, i).wait_send()
        for k in range(7):
            y_copy(k, e).wait_send()
    for k in range(8):
        for a in range(len(A_PARTS)):
            a_copy(k, a).wait_send()
        for b in range(len(B_PARTS)):
            b_copy(k, b).wait_send()


def body(tokens, norm_gain, running_sq, gate_weight, up_weight, down_weight_t, groups, cotangent):
    V = pltpu.VMEM
    any_spec = pl.BlockSpec(memory_space=pl.ANY)
    vmem_spec = pl.BlockSpec(memory_space=pltpu.VMEM)
    na, nb = len(A_PARTS), len(B_PARTS)
    sq = (128, 128)
    dma = pltpu.SemaphoreType.DMA
    scratch = [
        V((ROWS, FEAT), BF16), V((ROWS, FEAT), F32), V((NB, FEAT), F32), V((NB, FEAT), F32),
        V((2, ROWS, WIDTH), BF16), V((2, ROWS, WIDTH), BF16), V((2, WIDTH, 2 * ROWS), BF16),
        V((3, WIDTH, HALF), BF16), V((3, 2 * ROWS, HALF), BF16),
        V((ROWS, HALF), F32), V((ROWS, HALF), F32), V((2, ROWS, HALF), F32),
        V((2, 4, GROUPS, FEAT), BF16), V((2, 4, GROUPS, FEAT), BF16),
        V((na, WIDTH, 128), BF16), V((na, 1024, 128), BF16), V((na, 4, *sq), BF16),
        V((na, 4, 2, *sq), BF16), V((na, 2, *sq), BF16), V((na, 2, 2, *sq), BF16),
        V((nb, 4, 4, *sq), BF16), V((nb, 2, 2, *sq), BF16), V((nb, 2, 4, *sq), BF16),
        V((nb, 2, *sq), F32), V((nb, 2, *sq), BF16), V((nb, 2, *sq), BF16),
        V((nb, *sq), BF16), V((nb, *sq), BF16),
        V((2, 4, 2 * ROWS, FEAT), BF16), V((2, 4, 2 * ROWS, FEAT), BF16),
        V((2, 4, 2 * ROWS, FEAT), BF16), V((2, 2, ROWS, FEAT), BF16),
        V((2, 2, 2 * ROWS, FEAT), BF16), V((2, ROWS, FEAT), BF16), V((2, ROWS, FEAT), BF16),
        V((2, ROWS, FEAT), F32),
        dma((5,)), dma((2, 18)), dma((2, 18)), dma((2, 2, 4)), dma((2, 2, 4)),
        dma((8, na)), dma((8, na)), dma((8, nb)), dma((8, nb)), dma((2, 7)), dma((2, 7)),
        dma((2, 4)), dma((2, 4)),
    ]
    block_out, grad_tokens, run_new, gain_grad, grads = pl.pallas_call(
        kernel,
        out_shape=(
            jax.ShapeDtypeStruct((ROWS, FEAT), BF16),
            jax.ShapeDtypeStruct((ROWS, FEAT), BF16),
            jax.ShapeDtypeStruct((1, FEAT), F32),
            jax.ShapeDtypeStruct((1, FEAT), F32),
            jax.ShapeDtypeStruct((3, 128, 1024), F32),
        ),
        in_specs=[any_spec, vmem_spec, vmem_spec, any_spec, any_spec, any_spec, vmem_spec, any_spec],
        out_specs=(vmem_spec,) * 5,
        scratch_shapes=scratch,
        compiler_params=pltpu.CompilerParams(
            collective_id=0, has_side_effects=True, vmem_limit_bytes=67043328
        ),
    )(
        tokens, norm_gain.reshape(1, -1), running_sq.reshape(1, -1), gate_weight, up_weight,
        down_weight_t, groups.reshape(1, -1), cotangent,
    )
    return (
        block_out, grad_tokens, run_new.reshape(-1), gain_grad.reshape(-1),
        grads[1], grads[2], grads[0],
    )


def solution(mesh):
    placed = (
        P("tok", "mp"),
        P(),
        P("mp"),
        P(None, "mp"),
        P(None, "mp"),
        P(None, "mp"),
        P("tok"),
        P("tok", "mp"),
    )
    return jax.shard_map(
        body,
        mesh=mesh,
        in_specs=placed,
        out_specs=(
            P("tok", "mp"),
            P("tok", "mp"),
            P("mp"),
            P("mp"),
            P("tok", "mp"),
            P("tok", "mp"),
            P("tok", "mp"),
        ),
        check_vma=False,
    )
```

time: 234 us -> 99.2 us (0.42)
  waiting for transfers between devices: 105 us -> 0 us
  Pallas kernels: 0 us -> 89.1 us
  matrix products: 32.8 us -> 0 us
  starting transfers between devices: 29.9 us -> 0 us
  local copies, waits for them, and re-layouts: 31 us -> 8.21 us
  other arithmetic: 18.2 us -> 0 us
  between operations: 14.4 us -> 0.65 us
    pallas_call x0 -> x1, Pallas kernels: none -> 89.1 us  [body(): pl.pallas_call(kernel, out_shape=(jax.ShapeDtypeStruct((ROWS, FEAT), BF16...]
    all_to_all x6 -> x0, waiting for transfers between devices: 89 us -> none  [the longest x4 52.6 us: from_everyone(): return lax.all_to_all(copies, axis, split_axis=0, concat_axis=0, tiled=True)]
    dot_general x12 -> x0, matrix products: 32.8 us -> none  [the longest x3 10.1 us: contract_cols(): lax.dot_general(left, right, (((1,), (1,)), ((), ())), preferred_element_...]
    all_to_all x6 -> x0, starting transfers between devices: 29.9 us -> none  [the longest x4 22.4 us: from_everyone(): return lax.all_to_all(copies, axis, split_axis=0, concat_axis=0, tiled=True)]
    unnamed x46 -> x4, local copies, waits for them, and re-layouts: 23.2 us -> 5.66 us
    unnamed x2 -> x0, waiting for transfers between devices: 16.3 us -> none
    concatenate x1 -> x0, other arithmetic: 14.4 us -> none  [body(): jnp.concatenate([upper, lower], axis=1).astype(jnp.bfloat16)]
    broadcast_in_dim x4 -> x0, local copies, waits for them, and re-layouts: 4.33 us -> none  [from_everyone(): copies = jnp.broadcast_to(x, (lax.axis_size(axis), *x.shape))]
  transfers between devices with their start and end apart: 7 -> 0, of which waited for: 7 -> 0; matrix products, arithmetic and copies ran while one was open for 11% -> 0% of each run, Pallas kernels for 0% -> 0%
where the time goes in v2:
time: 99.2 us; the launch traced here: 98 us
  Pallas kernels  89.1 us (90%)
  local copies, waits for them, and re-layouts  8.21 us (8%)
    pallas_call x1, Pallas kernels, body(): pl.pallas_call(kernel, out_shape=(jax.ShapeDtypeStruct((ROWS, FEAT), BF16...  89.1 us
    unnamed x4, local copies, waits for them, and re-layouts  5.66 us
    squeeze x1, local copies, waits for them, and re-layouts, body(): grads[0]  2.55 us

profile of v2, /device:TPU:32, one launch (start us, length us, event | category | flops | bytes accessed | tf_op | source)
XLA Modules:
  0.0 98.0 jit_solution(2731738297919668163)
XLA Ops:
  0.6 89.1 %shard_map.135 = (bf16[384,256]{1,0:T(8,128)(2,1)}, bf16[384,256]{1,0:T(8,128)(2,1)}, f32[1,256]{1,0:T(1,128)}, f32[1,256]{1,0:T(1,128)}, f32[3,128,1024]{2,1,0:T(8,128)}) custom-call(bf16[384,256]{1,0:T(8,128)(2,1)} %tok_hbm.1, f32[1,2048]{1,0:T(1,128)} %bitcast.11, f32[1,256]{1,0:T(1,128)} %bitcast.12, bf16[2048,1024]{1,0:T(8,128)(2,1)} %gw_hbm.1, ...), custom_call_target="tpu_custom_call" | custom-call | tf_op jit(solution)/shard_map/pallas_call | solution.py:683
  89.8 2.5 %slice_bitcast_fusion = (f32[128,1024]{1,0:T(8,128)}, f32[128,1024]{1,0:T(8,128)}, f32[128,1024]{1,0:T(8,128)}) fusion(f32[3,128,1024]{2,1,0:T(8,128)} %get-tuple-element.16), kind=kLoop, calls=%fused_computation | loop fusion | bytes 3145728 | tf_op jit(solution)/shard_map/squeeze | solution.py:704
  92.3 1.6 %copy.19 = bf16[384,256]{1,0:T(8,128)(2,1)} copy(bf16[384,256]{1,0:T(8,128)(2,1)} %get-tuple-element.27) | data formatting | bytes 393216
  93.9 1.6 %copy.20 = bf16[384,256]{1,0:T(8,128)(2,1)} copy(bf16[384,256]{1,0:T(8,128)(2,1)} %get-tuple-element.28) | data formatting | bytes 393216
  95.5 1.2 %copy.21 = f32[256]{0:T(256)} copy(f32[256]{0:T(256)} %bitcast.14) | data formatting | bytes 2048
  96.7 1.2 %copy.22 = f32[256]{0:T(256)} copy(f32[256]{0:T(256)} %bitcast.13) | data formatting | bytes 2048

commit v3 on v2

--- a/solution.py
+++ b/solution.py
@@ -12,6 +12,7 @@
 WIDTH = 2048
 HALF = 512
 GROUPS = 48
+VMEM_LIMIT = 62 << 20
 NB = 24
 A_PARTS = tuple((p, 0) for p in range(5))
 B_PARTS = tuple((p, 1) for p in range(5)) + ((5, 0), (5, 1))
@@ -24,9 +25,9 @@
 
 
 def kernel(
-    tok_hbm, gain_ref, run_ref, gw_hbm, uw_hbm, dw_hbm, grp_ref, cot_hbm,
+    tok_hbm, gain_hbm, run_hbm, gw_hbm, uw_hbm, dw_hbm, grp_hbm, cot_hbm,
     bo_ref, gt_ref, rn_ref, gg_ref, gr_ref,
-    XT, NRM, BSUM, SCB, DYB, HB, LT, W, G, GT, LF, GH,
+    GR, GN, RN, XT, NRM, BSUM, SCB, DYB, HB, LT, W, G, GT, LF, GH,
     TZ, TX, PA, RSA, SPA, QA, R1, R2, PB, T1, T2, BK, BS, U1, BP, U2,
     EK, ES, ER, V1, V2, WS, W1, FS,
     lsem, gsend, grecv, ssend, srecv, asend, arecv, bsend, brecv, ysend, yrecv, csend, crecv,
@@ -54,10 +55,24 @@
 
     own_cols = pl.ds(pl.multiple_of(m * FEAT, FEAT), FEAT)
 
+    bar = pltpu.get_barrier_semaphore()
+    z_others = [(((z + k) % 4) * 4 + x, m) for k in range(1, 4)]
+    x_others = [(z * 4 + (x + k) % 4, m) for k in range(1, 4)]
+    for d in (*z_others, *x_others, dC, dYp, dYm):
+        pl.semaphore_signal(bar, inc=1, device_id=d, device_id_type=pl.DeviceIdType.MESH)
+
     cp_dy = pltpu.make_async_copy(cot_hbm, DYB.at[0, :, own_cols], lsem.at[0])
     cp_dy.start()
     cp_x = pltpu.make_async_copy(tok_hbm, XT, lsem.at[1])
     cp_x.start()
+    small = [
+        pltpu.make_async_copy(a, b, lsem.at[5 + i])
+        for i, (a, b) in enumerate(
+            ((grp_hbm, GR), (gain_hbm.at[:, own_cols], GN), (run_hbm, RN))
+        )
+    ]
+    for d in small:
+        d.start()
     wcols = pl.ds(pl.multiple_of(role * HALF, HALF), HALF)
     cp_w = [
         pltpu.make_async_copy(h.at[:, wcols], W.at[i], lsem.at[2 + i])
@@ -66,19 +81,14 @@
     for k in (2, 0, 1):
         cp_w[k].start()
 
-    bar = pltpu.get_barrier_semaphore()
-    z_others = [(((z + k) % 4) * 4 + x, m) for k in range(1, 4)]
-    x_others = [(z * 4 + (x + k) % 4, m) for k in range(1, 4)]
-    for d in (*z_others, *x_others, dC, dYp, dYm):
-        pl.semaphore_signal(bar, inc=1, device_id=d, device_id_type=pl.DeviceIdType.MESH)
-
     def sl(B, slot, yy, cc, r0=0, n=ROWS):
         return B.at[slot, pl.ds(r0, n), pl.ds(pl.multiple_of((yy * 2 + cc) * FEAT, FEAT), FEAT)]
 
     def gcopy(B, g, k):
         h = ROWS // 2
-        if k == 0:
-            a, b, d = sl(B, 0, y, c), sl(B, 1, y, c), dP
+        if k in (0, 18):
+            r = 0 if k == 0 else h
+            a, b, d = sl(B, 0, y, c, r, h), sl(B, 1, y, c, r, h), dP
         elif k in (1, 16):
             a = b = sl(B, 0, y, c, 0 if k == 1 else h, h)
             d = dYp
@@ -91,12 +101,9 @@
         elif k == 4:
             a = b = sl(B, 0, yp, c, h, h)
             d = dYm
-        elif k == 5:
-            a = b = sl(B, 1, y, c)
-            d = dYp
-        elif k == 6:
-            a = b = sl(B, 1, y, c)
-            d = dYm
+        elif k in (5, 6, 19, 20):
+            a = b = sl(B, 1, y, c, 0 if k < 7 else h, h)
+            d = dYp if k in (5, 19) else dYm
         elif k == 7:
             a, b, d = sl(B, 0, y2, c), sl(B, 1, y2, c), dP
         else:
@@ -108,8 +115,8 @@
 
     def gland(B, g, k):
         h = ROWS // 2
-        if k == 0:
-            b = sl(B, 1, y, c)
+        if k in (0, 18):
+            b = sl(B, 1, y, c, 0 if k == 0 else h, h)
         elif k in (1, 16):
             b = sl(B, 0, ym, c, 0 if k == 1 else h, h)
         elif k in (2, 17):
@@ -118,10 +125,8 @@
             b = sl(B, 0, y2, c, 0, h)
         elif k == 4:
             b = sl(B, 0, y2, c, h, h)
-        elif k == 5:
-            b = sl(B, 1, ym, c)
-        elif k == 6:
-            b = sl(B, 1, yp, c)
+        elif k in (5, 6, 19, 20):
+            b = sl(B, 1, ym if k in (5, 19) else yp, c, 0 if k < 7 else h, h)
         elif k == 7:
             b = sl(B, 1, y2, c)
         else:
@@ -131,9 +136,6 @@
     def gstart(B, g, *ks):
         for k in ks:
             gcopy(B, g, k).start()
-
-    def send_own(B, g):
-        gstart(B, g, 1, 2, 0, 16, 17, 8)
 
     def fwd(B, g, land, *sends):
         for k in land:
@@ -162,49 +164,56 @@
         TX[e, x] = tsum(e, 0).astype(BF16)
         tsend(e, 1)
 
-    grow = grp_ref[...]
-    onehot = (
-        lax.broadcasted_iota(jnp.int32, (GROUPS, NB), 0) == jnp.broadcast_to(grow, (GROUPS, NB))
-    ).astype(F32)
-    diag = lax.broadcasted_iota(jnp.int32, (NB, NB), 0) == lax.broadcasted_iota(
-        jnp.int32, (NB, NB), 1
-    )
-    gcol = jnp.sum(
-        jnp.where(diag, jnp.broadcast_to(grow, (NB, NB)), 0).astype(F32), axis=1, keepdims=True
-    )
-    onehot_t = (
-        lax.broadcasted_iota(jnp.int32, (NB, GROUPS), 1).astype(F32)
-        == jnp.broadcast_to(gcol, (NB, GROUPS))
-    ).astype(F32)
-
-    gain = gain_ref[:, own_cols]
+    def onehots():
+        grow = GR[...]
+        rows = lax.broadcasted_iota(jnp.int32, (GROUPS, NB), 0)
+        onehot = (rows == jnp.broadcast_to(grow, (GROUPS, NB))).astype(F32)
+        diag = lax.broadcasted_iota(jnp.int32, (NB, NB), 0) == lax.broadcasted_iota(
+            jnp.int32, (NB, NB), 1
+        )
+        gcol = jnp.sum(
+            jnp.where(diag, jnp.broadcast_to(grow, (NB, NB)), 0).astype(F32),
+            axis=1, keepdims=True,
+        )
+        onehot_t = (
+            lax.broadcasted_iota(jnp.int32, (NB, GROUPS), 1).astype(F32)
+            == jnp.broadcast_to(gcol, (NB, GROUPS))
+        ).astype(F32)
+        return onehot, onehot_t
 
     def start():
+        cp_dy.wait()
+        pl.semaphore_wait(bar, 9)
+        gstart(DYB, 0, 1, 2, 0, 16, 17, 8)
+
+    def stat0():
         cp_x.wait()
+        for d in small:
+            d.wait()
         for b in range(NB):
             xb = XT[b * BLK : (b + 1) * BLK, :].astype(F32)
             BSUM[b : b + 1, :] = jnp.sum(xb * xb, axis=0, keepdims=True)
         TZ[0, z] = jnp.dot(
-            onehot, BSUM[...], precision=HIGHEST, preferred_element_type=F32
+            onehots()[0], BSUM[...], precision=HIGHEST, preferred_element_type=F32
         ).astype(BF16)
-        cp_dy.wait()
-        pl.semaphore_wait(bar, 9)
         tsend(0, 0)
-        send_own(DYB, 0)
+        gstart(DYB, 0, 18)
 
     def stat2():
         quad = tsum(0, 1) / GHOST
-        rn_ref[...] = (1.0 - momentum) * run_ref[...] + momentum * (
+        rn_ref[...] = (1.0 - momentum) * RN[...] + momentum * (
             jnp.sum(quad, axis=0, keepdims=True) / GROUPS
         )
+        gain = GN[...]
         SCB[...] = jnp.dot(
-            onehot_t, lax.rsqrt(quad + epsilon), precision=HIGHEST, preferred_element_type=F32
+            onehots()[1], lax.rsqrt(quad + epsilon), precision=HIGHEST, preferred_element_type=F32
         )
         for b in range(NB):
             rows = slice(b * BLK, (b + 1) * BLK)
             nb = XT[rows, :].astype(F32) * SCB[b : b + 1, :]
             NRM[rows, :] = nb
             HB[0, rows, own_cols] = (gain * nb).astype(BF16)
+        gstart(HB, 1, 1, 2, 0, 18, 16, 17, 8)
 
     def transposed(B, i, slot):
         @pl.loop(0, 8)
@@ -212,18 +221,26 @@
             cols = pl.ds(pl.multiple_of(j * FEAT, FEAT), FEAT)
             LT[i, cols, pl.ds(slot * ROWS, ROWS)] = B[slot, :, cols].T
 
-    def units(slot):
+    def k_part(wi, slot, yy):
+        ks = pl.ds(pl.multiple_of(yy * 2 * FEAT, 2 * FEAT), 2 * FEAT)
+        return jnp.dot(HB[slot, :, ks], W[wi, ks, :], preferred_element_type=F32)
+
+    def units_a(slot):
         if slot == 0:
             cp_w[0].wait()
             cp_w[1].wait()
-        GT[...] = jnp.dot(HB[slot], W[0], preferred_element_type=F32)
-        LF[...] = jnp.dot(HB[slot], W[1], preferred_element_type=F32)
-
-        @pl.loop(0, ROWS // 16)
+        for wi, dst in ((0, GT), (1, LF)):
+            dst[slot] = k_part(wi, slot, y) + k_part(wi, slot, ym) + k_part(wi, slot, yp)
+
+    def units_b(slot):
+        GT[slot] += k_part(0, slot, y2)
+        LF[slot] += k_part(1, slot, y2)
+
+        @pl.loop(0, ROWS // 32)
         def _(i):
-            r = pl.ds(pl.multiple_of(i * 16, 16), 16)
-            ro = pl.ds(pl.multiple_of(slot * ROWS + i * 16, 16), 16)
-            gate, lift, gh = GT[r, :], LF[r, :], GH[slot, r, :]
+            r = pl.ds(pl.multiple_of(i * 32, 32), 32)
+            ro = pl.ds(pl.multiple_of(slot * ROWS + i * 32, 32), 32)
+            gate, lift, gh = GT[slot, r, :], LF[slot, r, :], GH[slot, r, :]
             sigma = jax.nn.sigmoid(gate)
             G[0, ro, :] = (gate * sigma * lift).astype(BF16)
             G[1, ro, :] = (gh * lift * sigma * (1.0 + gate * (1.0 - sigma))).astype(BF16)
@@ -234,8 +251,8 @@
             cp_w[2].wait()
         GH[slot] = jnp.dot(DYB[slot], W[2], preferred_element_type=F32)
 
-    def slot_ready(B, g, slot):
-        for k in range(8 + 4 * slot, 12 + 4 * slot):
+    def ready(B, g, *ks):
+        for k in ks:
             gland(B, g, k)
 
     AS, AP, AX1P, AX1M, AXIP, AXIM, AX2P, AX2M = range(8)
@@ -288,7 +305,8 @@
         mi, j = p // 2, p % 2
 
         @pl.loop(0, 2)
-        def _(rh):
+        def _(n):
+            rh = (1 - pair + n) % 2
             rows = pl.ds(pl.multiple_of(rh * 1024, 1024), 1024)
             res = jnp.dot(
                 LT[(mi + 1) // 2, rows, :],
@@ -304,9 +322,12 @@
                     for i in range(8):
                         PB[b, i % 4, rh * 2 + i // 4] = part[i * 128 : (i + 1) * 128]
 
-        for off in range(2):
-            if (p, off) in A_PARTS:
-                a_copy(AS, A_PARTS.index((p, off))).start()
+            @pl.when(n == 0)
+            def _():
+                for off in range(2):
+                    if (p, off) in A_PARTS:
+                        a_copy(AS, A_PARTS.index((p, off))).start()
+
         for ks in ((BX1P, BX1M), (BXIP, BXIM)):
             for off in range(2):
                 if (p, off) in B_PARTS:
@@ -494,15 +515,16 @@
             FS[0, rows, :] = g
             BSUM[b : b + 1, :] = jnp.sum(g * NRM[rows, :], axis=0, keepdims=True)
         TZ[1, z] = jnp.dot(
-            onehot, BSUM[...], precision=HIGHEST, preferred_element_type=F32
+            onehots()[0], BSUM[...], precision=HIGHEST, preferred_element_type=F32
         ).astype(BF16)
         tsend(1, 0)
 
     def y_grad_tokens():
         total = tsum(1, 1)
         gg_ref[...] = jnp.sum(total, axis=0, keepdims=True)
+        gain = GN[...]
         BSUM[...] = jnp.dot(
-            onehot_t, gain * total / GHOST, precision=HIGHEST, preferred_element_type=F32
+            onehots()[1], gain * total / GHOST, precision=HIGHEST, preferred_element_type=F32
         )
         for b in range(NB):
             rows = slice(b * BLK, (b + 1) * BLK)
@@ -513,131 +535,139 @@
             ).astype(BF16)
 
     start()
-    tmid(0)
+    stat0()
     fwd(DYB, 0, (2,), 4)
     fwd(DYB, 0, (1,), 3)
+    fwd(DYB, 0, (0,), 5, 6)
+    tmid(0)
     fwd(DYB, 0, (16,), 9)
     fwd(DYB, 0, (17,), 10)
-    fwd(DYB, 0, (0,), 5, 6, 12)
+    fwd(DYB, 0, (18,), 19, 20, 12)
+    fwd(DYB, 0, (3, 4), 7, 11)
     stat2()
-    fwd(DYB, 0, (3, 4), 7, 11)
-    send_own(HB, 1)
-    slot_ready(DYB, 0, 0)
+    ready(DYB, 0, 8, 9, 10)
+    ready(DYB, 0, 11)
+    transposed(DYB, 0, 0)
     gh(0)
-    transposed(DYB, 0, 0)
-    fwd(DYB, 0, (6,), 14)
-    fwd(DYB, 0, (5,), 13)
+    fwd(DYB, 0, (6, 20), 14)
+    fwd(DYB, 0, (5, 19), 13)
     fwd(DYB, 0, (7,), 15)
+    fwd(HB, 1, (2,), 4)
     fwd(HB, 1, (1,), 3)
-    fwd(HB, 1, (2,), 4)
-    slot_ready(DYB, 0, 1)
+    ready(DYB, 0, 12, 13, 14)
+    ready(DYB, 0, 15)
+    gh(1)
+    fwd(HB, 1, (0,), 5, 6)
+    fwd(HB, 1, (16,), 9)
     transposed(DYB, 0, 1)
-    gh(1)
-    fwd(HB, 1, (16,), 9)
     fwd(HB, 1, (17,), 10)
-    fwd(HB, 1, (0,), 5, 6, 12)
+    fwd(HB, 1, (18,), 19, 20, 12)
     fwd(HB, 1, (3, 4), 7, 11)
-    slot_ready(HB, 1, 0)
-    units(0)
+    ready(HB, 1, 8, 9, 10)
+    units_a(0)
+    ready(HB, 1, 11)
     transposed(HB, 1, 0)
-    fwd(HB, 1, (6,), 14)
-    fwd(HB, 1, (5,), 13)
+    units_b(0)
+    fwd(HB, 1, (5, 19), 13)
+    fwd(HB, 1, (6, 20), 14)
     fwd(HB, 1, (7,), 15)
-    slot_ready(HB, 1, 1)
-    units(1)
+    ready(HB, 1, 12, 13, 14)
+    units_a(1)
+    ready(HB, 1, 15)
+    units_b(1)
     weights(0)
+    y_own(1, 2)
     y_sib(0, 0)
-    y_sib(1, 3)
-    y_sib(0, 2)
-    y_sib(1, 1)
     weights(1)
     y_own(0, 0)
+    step_bx2(0)
     y_merge(0, 0, V1P, V1M)
+    transposed(HB, 1, 1)
+    y_sib(1, 1)
+    weights(4)
+    y_sib(0, 2)
+    weights(3)
+    step_ap(0)
     y_sib(0, 1)
-    y_own(0, 1)
-    y_own(1, 3)
-    transposed(HB, 1, 1)
-    weights(5)
-    y_merge(0, 1, VIP)
-    weights(2)
-    step_bx2(1)
-    y_own(0, 3)
-    y_sib(1, 0)
-    y_own(1, 0)
-    y_sib(1, 2)
     y_own(0, 2)
     y_merge(0, 2, VIM)
     y_relay(0, 1)
-    step_bx2(5)
+    step_bx2(4)
+    y_own(0, 1)
+    y_merge(0, 1, VIP)
     y_relay(0, 0)
-    step_ap(0)
-    step_bx2(0)
+    weights(2)
+    step_bx2(3)
+    step_ap(1)
+    y_sib(1, 0)
+    step_bs(0)
+    y_own(1, 0)
+    y_sib(1, 3)
     y_sib(0, 3)
-    weights(4)
+    step_bs(4)
+    step_bx2(1)
+    y_own(1, 3)
+    y_sib(1, 2)
+    step_bx2(2)
     y_merge(1, 0, V1P, V1M)
-    step_bx2(6)
-    y_own(1, 2)
-    y_merge(1, 2, VIM)
+    weights(5)
+    step_ap(4)
+    step_ax1(1)
+    step_ax1(0)
     y_own(1, 1)
     y_merge(1, 1, VIP)
+    y_merge(1, 2, VIM)
+    y_own(0, 3)
     y_merge(0, 3)
+    step_bs(3)
     y_merge(1, 3)
-    step_ap(1)
-    weights(3)
-    step_ax1(0)
-    step_bx2(2)
-    step_ax1(1)
+    y_p(0)
     step_bs(1)
+    y_f(0)
+    step_bs(2)
+    step_ax1(4)
+    step_bx2(5)
+    step_ap(3)
+    y_relay(1, 1)
+    step_bx2(6)
+    y_relay(1, 0)
+    y_partial()
+    step_ax2(1)
     step_ap(2)
+    step_ax2(0)
+    step_ax1(3)
+    step_bp(0)
+    step_ax2(4)
+    step_bp(4)
+    y_p(1)
     step_bs(5)
-    y_p(0)
-    y_f(0)
-    step_bs(0)
-    y_relay(1, 0)
-    step_bx2(4)
+    step_bp(3)
     step_ax1(2)
-    step_ap(4)
-    y_relay(1, 1)
+    y_f(1)
     step_bs(6)
-    step_bx2(3)
-    y_partial()
-    step_ax2(0)
-    step_ap(3)
-    step_ax1(4)
-    step_bs(2)
+    step_bf(0)
     step_bp(1)
-    step_ax2(1)
-    step_bp(5)
-    y_p(1)
-    y_f(1)
-    step_bs(4)
-    step_bp(0)
-    step_ax2(2)
-    step_ax1(3)
-    step_bf(1)
-    step_bp(6)
-    tmid(1)
-    step_bf(5)
-    step_bs(3)
+    step_af(1)
+    step_bf(4)
     step_af(0)
     step_bp(2)
-    step_ax2(4)
-    step_bp(4)
-    step_af(1)
-    step_af(2)
-    step_bp(3)
+    step_ax2(3)
+    tmid(1)
+    step_af(4)
+    step_bp(5)
+    step_ax2(2)
+    step_bp(6)
     y_block_out()
-    step_ax2(3)
-    step_bf(0)
-    step_bf(6)
-    step_bf(2)
-    step_af(4)
-    y_grad_tokens()
-    step_bf(4)
     step_af(3)
     step_bf(3)
+    step_bf(1)
+    step_bf(2)
+    step_af(2)
+    y_grad_tokens()
+    step_bf(5)
+    step_bf(6)
     for g, B in ((0, DYB), (1, HB)):
-        for k in range(18):
+        for k in range(21):
             gcopy(B, g, k).wait_send()
     for e in range(2):
         for a in range(2):
@@ -654,6 +684,20 @@
             b_copy(k, b).wait_send()
 
 
+def emit(bo_ref, gt_ref, rn_ref, gg_ref, gr_ref, bo, gt, rn, gg, g_gate, g_up, g_down, sem):
+    copies = [
+        pltpu.make_async_copy(a, b, sem.at[i])
+        for i, (a, b) in enumerate((
+            (gr_ref.at[1], g_gate), (gr_ref.at[2], g_up), (gr_ref.at[0], g_down),
+            (bo_ref, bo), (gt_ref, gt), (rn_ref, rn), (gg_ref, gg),
+        ))
+    ]
+    for d in copies:
+        d.start()
+    for d in copies:
+        d.wait()
+
+
 def body(tokens, norm_gain, running_sq, gate_weight, up_weight, down_weight_t, groups, cotangent):
     V = pltpu.VMEM
     any_spec = pl.BlockSpec(memory_space=pl.ANY)
@@ -662,10 +706,11 @@
     sq = (128, 128)
     dma = pltpu.SemaphoreType.DMA
     scratch = [
+        V((1, NB), jnp.int32), V((1, FEAT), F32), V((1, FEAT), F32),
         V((ROWS, FEAT), BF16), V((ROWS, FEAT), F32), V((NB, FEAT), F32), V((NB, FEAT), F32),
         V((2, ROWS, WIDTH), BF16), V((2, ROWS, WIDTH), BF16), V((2, WIDTH, 2 * ROWS), BF16),
         V((3, WIDTH, HALF), BF16), V((3, 2 * ROWS, HALF), BF16),
-        V((ROWS, HALF), F32), V((ROWS, HALF), F32), V((2, ROWS, HALF), F32),
+        V((2, ROWS, HALF), F32), V((2, ROWS, HALF), F32), V((2, ROWS, HALF), F32),
         V((2, 4, GROUPS, FEAT), BF16), V((2, 4, GROUPS, FEAT), BF16),
         V((na, WIDTH, 128), BF16), V((na, 1024, 128), BF16), V((na, 4, *sq), BF16),
         V((na, 4, 2, *sq), BF16), V((na, 2, *sq), BF16), V((na, 2, 2, *sq), BF16),
@@ -676,32 +721,38 @@
         V((2, 4, 2 * ROWS, FEAT), BF16), V((2, 2, ROWS, FEAT), BF16),
         V((2, 2, 2 * ROWS, FEAT), BF16), V((2, ROWS, FEAT), BF16), V((2, ROWS, FEAT), BF16),
         V((2, ROWS, FEAT), F32),
-        dma((5,)), dma((2, 18)), dma((2, 18)), dma((2, 2, 4)), dma((2, 2, 4)),
+        dma((8,)), dma((2, 21)), dma((2, 21)), dma((2, 2, 4)), dma((2, 2, 4)),
         dma((8, na)), dma((8, na)), dma((8, nb)), dma((8, nb)), dma((2, 7)), dma((2, 7)),
         dma((2, 4)), dma((2, 4)),
     ]
-    block_out, grad_tokens, run_new, gain_grad, grads = pl.pallas_call(
+    held = (
+        ((ROWS, FEAT), BF16), ((ROWS, FEAT), BF16), ((1, FEAT), F32), ((1, FEAT), F32),
+        ((3, 128, 1024), F32),
+    )
+    results = pl.pallas_call(
         kernel,
-        out_shape=(
-            jax.ShapeDtypeStruct((ROWS, FEAT), BF16),
-            jax.ShapeDtypeStruct((ROWS, FEAT), BF16),
-            jax.ShapeDtypeStruct((1, FEAT), F32),
-            jax.ShapeDtypeStruct((1, FEAT), F32),
-            jax.ShapeDtypeStruct((3, 128, 1024), F32),
-        ),
-        in_specs=[any_spec, vmem_spec, vmem_spec, any_spec, any_spec, any_spec, vmem_spec, any_spec],
+        out_shape=tuple(pltpu.VMEM(shape, dtype) for shape, dtype in held),
+        in_specs=[any_spec] * 8,
         out_specs=(vmem_spec,) * 5,
         scratch_shapes=scratch,
         compiler_params=pltpu.CompilerParams(
-            collective_id=0, has_side_effects=True, vmem_limit_bytes=67043328
+            collective_id=0, has_side_effects=True, vmem_limit_bytes=VMEM_LIMIT
         ),
     )(
         tokens, norm_gain.reshape(1, -1), running_sq.reshape(1, -1), gate_weight, up_weight,
         down_weight_t, groups.reshape(1, -1), cotangent,
     )
+    weight = jax.ShapeDtypeStruct((128, 1024), F32)
+    block_out, grad_tokens, run_new, gain_grad, g_gate, g_up, g_down = pl.pallas_call(
+        emit,
+        out_shape=tuple(jax.ShapeDtypeStruct(*a) for a in held[:4]) + (weight,) * 3,
+        in_specs=[vmem_spec] * 5,
+        out_specs=(any_spec,) * 7,
+        scratch_shapes=[dma((7,))],
+        compiler_params=pltpu.CompilerParams(vmem_limit_bytes=4 << 20),
+    )(*results)
     return (
-        block_out, grad_tokens, run_new.reshape(-1), gain_grad.reshape(-1),
-        grads[1], grads[2], grads[0],
+        block_out, grad_tokens, run_new.reshape(-1), gain_grad.reshape(-1), g_gate, g_up, g_down,
     )
 
 

time: 99.2 us -> 85.6 us (0.86)
  local copies, waits for them, and re-layouts: 8.21 us -> 0 us
  Pallas kernels: 89.1 us -> 83.5 us
    unnamed x4 -> x0, local copies, waits for them, and re-layouts: 5.66 us -> none
    pallas_call x1 -> x2, Pallas kernels: 89.1 us -> 83.5 us  [the longest x1 82.2 us: body(): pl.pallas_call(kernel, out_shape=tuple((pltpu.VMEM(shape, dtype) for shap...]
    squeeze x1 -> x0, local copies, waits for them, and re-layouts: 2.55 us -> none  [body(): grads[0]]
where the time goes in v3:
time: 85.6 us; the launch traced here: 84.3 us
  Pallas kernels  83.5 us (98%)
    pallas_call x1, Pallas kernels, body(): pl.pallas_call(kernel, out_shape=tuple((pltpu.VMEM(shape, dtype) for shap...  82.2 us

profile of v3, /device:TPU:32, one launch (start us, length us, event | category | flops | bytes accessed | tf_op | source)
XLA Modules:
  0.0 84.3 jit_solution(9541491639173825574)
XLA Ops:
  0.6 82.2 %shard_map.135 = (bf16[384,256]{1,0:T(8,128)(2,1)S(1)}, bf16[384,256]{1,0:T(8,128)(2,1)S(1)}, f32[1,256]{1,0:T(1,128)S(1)}, f32[1,256]{1,0:T(1,128)S(1)}, f32[3,128,1024]{2,1,0:T(8,128)S(1)}) custom-call(bf16[384,256]{1,0:T(8,128)(2,1)} %tok_hbm.1, f32[1,2048]{1,0:T(1,128)} %bitcast.5, f32[1,256]{1,0:T(1,128)} %bitcast.6, bf16[2048,1024]{1,0:T(8,128)(2,1)} %gw_hbm.1, ...), custom_call_target="tpu_custom_call" | custom-call | tf_op jit(solution)/shard_map/pallas_call | solution.py:732
  82.8 1.3 %shard_map.136 = (bf16[384,256]{1,0:T(8,128)(2,1)}, bf16[384,256]{1,0:T(8,128)(2,1)}, f32[1,256]{1,0:T(1,128)}, f32[1,256]{1,0:T(1,128)}, f32[128,1024]{1,0:T(8,...) custom-call(bf16[384,256]{1,0:T(8,128)(2,1)S(1)} %get-tuple-element.19.bo_ref, ...), custom_call_target="tpu_custom_call" | custom-call | tf_op jit(solution)/shard_map/pallas_call | solution.py:746

commit v4 on v3

--- a/solution.py
+++ b/solution.py
@@ -12,6 +12,7 @@
 WIDTH = 2048
 HALF = 512
 GROUPS = 48
+G_SEM = (0, 1, 2, 3, 3, 4, 5, 6, 7, 8, 9, 10, 11, 12, 13, 14, 15, 16, 17, 4, 5)
 VMEM_LIMIT = 62 << 20
 NB = 24
 A_PARTS = tuple((p, 0) for p in range(5))
@@ -111,7 +112,7 @@
             yy = (y, ym, yp, y2)[(k - 8) % 4]
             a = b = sl(B, slot, yy, c)
             d = dC
-        return rc(a, b, gsend.at[g, k], grecv.at[g, k], d)
+        return rc(a, b, gsend.at[g], grecv.at[g, G_SEM[k]], d)
 
     def gland(B, g, k):
         h = ROWS // 2
@@ -122,16 +123,16 @@
         elif k in (2, 17):
             b = sl(B, 0, yp, c, h if k == 2 else 0, h)
         elif k == 3:
-            b = sl(B, 0, y2, c, 0, h)
-        elif k == 4:
-            b = sl(B, 0, y2, c, h, h)
-        elif k in (5, 6, 19, 20):
-            b = sl(B, 1, ym if k in (5, 19) else yp, c, 0 if k < 7 else h, h)
+            b = sl(B, 0, y2, c)
+        elif k == 5:
+            b = sl(B, 1, ym, c)
+        elif k == 6:
+            b = sl(B, 1, yp, c)
         elif k == 7:
             b = sl(B, 1, y2, c)
         else:
             b = sl(B, (k - 8) // 4, (y, ym, yp, y2)[(k - 8) % 4], 1 - c)
-        rc(b, b, gsend.at[g, k], grecv.at[g, k], dC).wait_recv()
+        rc(b, b, gsend.at[g], grecv.at[g, G_SEM[k]], dC).wait_recv()
 
     def gstart(B, g, *ks):
         for k in ks:
@@ -145,13 +146,13 @@
     def tcopy(e, a, k):
         buf, me, d = ((TZ, z, z_others), (TX, x, x_others))[a]
         ref = buf.at[e, me]
-        return rc(ref, ref, ssend.at[e, a, k], srecv.at[e, a, k], d[k - 1])
+        return rc(ref, ref, ssend.at[e], srecv.at[e, a, k - 1], d[k - 1])
 
     def tsum(e, a):
         buf, me = ((TZ, z), (TX, x))[a]
         for k in range(1, 4):
             ref = buf.at[e, (me + 4 - k) % 4]
-            rc(ref, ref, ssend.at[e, a, k], srecv.at[e, a, k], dC).wait_recv()
+            rc(ref, ref, ssend.at[e], srecv.at[e, a, k - 1], dC).wait_recv()
         return (buf[e, 0].astype(F32) + buf[e, 1].astype(F32)) + (
             buf[e, 2].astype(F32) + buf[e, 3].astype(F32)
         )
@@ -184,7 +185,7 @@
     def start():
         cp_dy.wait()
         pl.semaphore_wait(bar, 9)
-        gstart(DYB, 0, 1, 2, 0, 16, 17, 8)
+        gstart(DYB, 0, 1, 2, 16, 17, 8)
 
     def stat0():
         cp_x.wait()
@@ -197,7 +198,7 @@
             onehots()[0], BSUM[...], precision=HIGHEST, preferred_element_type=F32
         ).astype(BF16)
         tsend(0, 0)
-        gstart(DYB, 0, 18)
+        gstart(DYB, 0, 0, 18)
 
     def stat2():
         quad = tsum(0, 1) / GHOST
@@ -225,17 +226,16 @@
         ks = pl.ds(pl.multiple_of(yy * 2 * FEAT, 2 * FEAT), 2 * FEAT)
         return jnp.dot(HB[slot, :, ks], W[wi, ks, :], preferred_element_type=F32)
 
-    def units_a(slot):
-        if slot == 0:
+    def k_block(slot, i, first):
+        yy = (y, ym, yp, y2)[i]
+        if first and slot == 0:
             cp_w[0].wait()
             cp_w[1].wait()
         for wi, dst in ((0, GT), (1, LF)):
-            dst[slot] = k_part(wi, slot, y) + k_part(wi, slot, ym) + k_part(wi, slot, yp)
-
-    def units_b(slot):
-        GT[slot] += k_part(0, slot, y2)
-        LF[slot] += k_part(1, slot, y2)
-
+            v = k_part(wi, slot, yy)
+            dst[slot] = v if first else dst[slot] + v
+
+    def units(slot):
         @pl.loop(0, ROWS // 32)
         def _(i):
             r = pl.ds(pl.multiple_of(i * 32, 32), 32)
@@ -257,6 +257,8 @@
 
     AS, AP, AX1P, AX1M, AXIP, AXIM, AX2P, AX2M = range(8)
     BX1P, BX1M, BXIP, BXIM, BX2P, BX2M, BSK, BPK = range(8)
+    A_SEM = (0, 1, 2, 2, 3, 3, 3, 3)
+    B_SEM = (0, 0, 1, 1, 1, 1, 2, 3)
     pair = z // 2
     lo2, hi2 = pl.ds(0, 2), pl.ds(2, 2)
 
@@ -272,14 +274,11 @@
             (QA.at[a, xp, 0], R2.at[a, 0, 0], dXp),
             (QA.at[a, xm, 1], R2.at[a, 1, 1], dXm),
         )[k]
-        return rc(src, dst, asend.at[k, a], arecv.at[k, a], d)
-
-    def a_land(k, a):
-        b = (
-            RSA.at[a], QA.at[a, :, 1 - role], R1.at[a, 0], R1.at[a, 1],
-            R2.at[a, 0, 1], R2.at[a, 1, 0], R2.at[a, 0, 0], R2.at[a, 1, 1],
-        )[k]
-        rc(b, b, asend.at[k, a], arecv.at[k, a], dC).wait_recv()
+        return rc(src, dst, asend.at[a], arecv.at[A_SEM[k], a], d)
+
+    def a_land(n, a):
+        b = (RSA.at[a], QA.at[a, :, 1 - role], R1.at[a], R2.at[a])[n]
+        rc(b, b, asend.at[a], arecv.at[n, a], dC).wait_recv()
 
     def b_copy(k, b):
         src, dst, d = (
@@ -292,14 +291,11 @@
             (BS.at[b], U1.at[b], dS),
             (BP.at[b], U2.at[b], dP),
         )[k]
-        return rc(src, dst, bsend.at[k, b], brecv.at[k, b], d)
-
-    def b_land(k, b):
-        r = (
-            T1.at[b, 0], T1.at[b, 1], T2.at[b, 0, hi2], T2.at[b, 1, lo2],
-            T2.at[b, 0, lo2], T2.at[b, 1, hi2], U1.at[b], U2.at[b],
-        )[k]
-        rc(r, r, bsend.at[k, b], brecv.at[k, b], dC).wait_recv()
+        return rc(src, dst, bsend.at[b], brecv.at[B_SEM[k], b], d)
+
+    def b_land(n, b):
+        r = (T1.at[b], T2.at[b], U1.at[b], U2.at[b])[n]
+        rc(r, r, bsend.at[b], brecv.at[n, b], dC).wait_recv()
 
     def weights(p):
         mi, j = p // 2, p % 2
@@ -342,7 +338,7 @@
         return pl.ds(pl.multiple_of(half * HALF + (p % 2) * 256 + off * 128, 128), 128)
 
     def step_ap(a):
-        a_land(AS, a)
+        a_land(0, a)
         for xd in range(4):
             ra = pl.ds(pl.multiple_of(zp * HALF + xd * 128, 128), 128)
             rr = pl.ds(pl.multiple_of((zp % 2) * HALF + xd * 128, 128), 128)
@@ -354,39 +350,35 @@
             QA[a, xd, role] = plus(PA[a, ra, :], RSA[a, rr, :]).astype(BF16)
 
     def step_ax1(a):
-        a_land(AP, a)
+        a_land(1, a)
         for k in (AX1P, AX1M, AXIP, AXIM):
             a_copy(k, a).start()
 
     def step_ax2(a):
-        a_land(AX1P, a)
+        a_land(2, a)
         QA[a, xp, 0] = plus(QA[a, xp, 0], R1[a, 0]).astype(BF16)
         a_copy(AX2P, a).start()
-        a_land(AX1M, a)
         QA[a, xm, 1] = plus(QA[a, xm, 1], R1[a, 1]).astype(BF16)
         a_copy(AX2M, a).start()
 
     def step_af(a):
-        for k in (AXIP, AXIM, AX2P, AX2M):
-            a_land(k, a)
+        a_land(3, a)
         for h in range(2):
             gr_ref[A_PARTS[a][0] // 2, :, out_cols(A_PARTS[a], h)] = plus(
                 QA[a, x, h], R2[a, 0, h]
             ) + R2[a, 1, h].astype(F32)
 
     def step_bx2(b):
-        b_land(BX1P, b)
+        b_land(0, b)
         for i in range(2):
             PB[b, xp, i] = plus(PB[b, xp, i], T1[b, 0, i]).astype(BF16)
         b_copy(BX2P, b).start()
-        b_land(BX1M, b)
         for i in range(2):
             PB[b, xm, 2 + i] = plus(PB[b, xm, 2 + i], T1[b, 1, i]).astype(BF16)
         b_copy(BX2M, b).start()
 
     def step_bs(b):
-        for k in (BXIP, BXIM, BX2P, BX2M):
-            b_land(k, b)
+        b_land(1, b)
         for i in range(2):
             o = 2 * (1 - pair) + i
             BS[b, i] = (plus(PB[b, x, o], T2[b, 0, o]) + T2[b, 1, o].astype(F32)).astype(BF16)
@@ -396,7 +388,7 @@
             BK[b, i] = plus(PB[b, x, o], T2[b, 0, o]) + T2[b, 1, o].astype(F32)
 
     def step_bp(b):
-        b_land(BSK, b)
+        b_land(2, b)
         BP[b] = plus(BK[b, zp % 2], U1[b, zp % 2]).astype(BF16)
         b_copy(BPK, b).start()
         gr_ref[B_PARTS[b][0] // 2, :, out_cols(B_PARTS[b], role)] = plus(
@@ -404,12 +396,13 @@
         )
 
     def step_bf(b):
-        b_land(BPK, b)
+        b_land(3, b)
         gr_ref[B_PARTS[b][0] // 2, :, out_cols(B_PARTS[b], 1 - role)] = U2[b].astype(F32)
 
     V1P, V1M, VIP, VIM, V2P, V2M, WSK = range(7)
     lo, hi = pl.ds(0, ROWS), pl.ds(ROWS, ROWS)
     y_of = (y2, yp, ym, y)
+    Y_SEM = (0, 1, 2, 3, 3, 2, 4)
 
     def y_copy(k, e):
         a, b, d = (
@@ -421,18 +414,15 @@
             (EK.at[e, ym, hi], V2.at[e, 1, hi], dYm),
             (WS.at[e], W1.at[e], dP),
         )[k]
-        return rc(a, b, ysend.at[e, k], yrecv.at[e, k], d)
-
-    def y_land(k, e):
-        b = (
-            V1.at[e, 0], V1.at[e, 1], V2.at[e, 0, hi], V2.at[e, 1, lo],
-            V2.at[e, 0, lo], V2.at[e, 1, hi], W1.at[e],
-        )[k]
-        rc(b, b, ysend.at[e, k], yrecv.at[e, k], dC).wait_recv()
+        return rc(a, b, ysend.at[e], yrecv.at[e, Y_SEM[k]], d)
+
+    def y_land(n, e):
+        b = (V1.at[e, 0], V1.at[e, 1], V2.at[e, :, hi], V2.at[e, :, lo], W1.at[e])[n]
+        rc(b, b, ysend.at[e], yrecv.at[e, n], dC).wait_recv()
 
     def sib_copy(e, i):
         return rc(
-            ES.at[e, y_of[i]], ER.at[e, y_of[i]], csend.at[e, i], crecv.at[e, i], dC
+            ES.at[e, y_of[i]], ER.at[e, y_of[i]], csend.at[e], crecv.at[e, i], dC
         )
 
     def nt(a, b):
@@ -466,7 +456,7 @@
             y_copy(k, e).start()
 
     def y_relay(e, d):
-        y_land((V1P, V1M)[d], e)
+        y_land(d, e)
         yy = (yp, ym)[d]
 
         @pl.loop(0, 3)
@@ -478,8 +468,7 @@
         y_copy((V2P, V2M)[d], e).start()
 
     def y_p(e):
-        y_land(VIP, e)
-        y_land(V2M, e)
+        y_land(2, e)
 
         @pl.loop(0, 3)
         def _(n):
@@ -492,8 +481,7 @@
         y_copy(WSK, e).start()
 
     def y_f(e):
-        y_land(VIM, e)
-        y_land(V2P, e)
+        y_land(3, e)
 
         @pl.loop(0, 3)
         def _(n):
@@ -501,14 +489,14 @@
             FS[e, r, :] = plus(EK[e, y, r, :], V2[e, 0, r, :]) + V2[e, 1, r, :].astype(F32)
 
     def y_block_out():
-        y_land(WSK, 1)
+        y_land(4, 1)
         for b in range(NB):
             rows = slice(b * BLK, (b + 1) * BLK)
             branch = FS[1, rows, :] + W1[1, rows, :].astype(F32)
             bo_ref[rows, :] = (XT[rows, :].astype(F32) + branch).astype(BF16)
 
     def y_partial():
-        y_land(WSK, 0)
+        y_land(4, 0)
         for b in range(NB):
             rows = slice(b * BLK, (b + 1) * BLK)
             g = FS[0, rows, :] + W1[0, rows, :].astype(F32)
@@ -534,154 +522,190 @@
                 dyb + SCB[b : b + 1, :] * (gain * g - nb * BSUM[b : b + 1, :])
             ).astype(BF16)
 
+    def left(sem, kib):
+        ref = LT.at[0, pl.ds(0, kib * 1024 // (4 * ROWS))]
+        rc(ref, ref, sem, sem, dC).wait_send()
+
+    def left_gather(B, g):
+        left(gsend.at[g], 30 * 96)
+
+    def left_table(e):
+        left(ssend.at[e], 6 * 24)
+
+    def left_sums(e):
+        left(csend.at[e], 4 * 384)
+        left(ysend.at[e], 7 * 192)
+
+    def left_a(a):
+        left(asend.at[a], 18 * 32)
+
+    def left_b(b):
+        left(bsend.at[b], 15 * 32)
+
     start()
     stat0()
+    tmid(0)
     fwd(DYB, 0, (2,), 4)
     fwd(DYB, 0, (1,), 3)
     fwd(DYB, 0, (0,), 5, 6)
-    tmid(0)
     fwd(DYB, 0, (16,), 9)
     fwd(DYB, 0, (17,), 10)
-    fwd(DYB, 0, (18,), 19, 20, 12)
-    fwd(DYB, 0, (3, 4), 7, 11)
     stat2()
-    ready(DYB, 0, 8, 9, 10)
-    ready(DYB, 0, 11)
+    gland(DYB, 0, 8)
+    fwd(DYB, 0, (3,), 7, 11)
+    gland(DYB, 0, 9)
+    gland(DYB, 0, 10)
+    gland(HB, 1, 8)
+    k_block(0, 0, True)
+    gland(DYB, 0, 11)
     transposed(DYB, 0, 0)
     gh(0)
-    fwd(DYB, 0, (6, 20), 14)
-    fwd(DYB, 0, (5, 19), 13)
+    fwd(HB, 1, (1,), 3)
+    fwd(HB, 1, (2,), 4)
+    fwd(DYB, 0, (18,), 19, 20, 12)
+    fwd(HB, 1, (0,), 5, 6)
+    gland(DYB, 0, 12)
+    fwd(HB, 1, (18,), 19, 20, 12)
+    fwd(HB, 1, (17,), 10)
+    fwd(HB, 1, (16,), 9)
+    gland(HB, 1, 12)
+    k_block(1, 0, True)
+    gland(HB, 1, 10)
+    k_block(0, 2, False)
+    fwd(HB, 1, (3,), 7, 11)
+    gland(HB, 1, 9)
+    k_block(0, 1, False)
     fwd(DYB, 0, (7,), 15)
-    fwd(HB, 1, (2,), 4)
-    fwd(HB, 1, (1,), 3)
-    ready(DYB, 0, 12, 13, 14)
-    ready(DYB, 0, 15)
+    fwd(DYB, 0, (5,), 13)
+    fwd(DYB, 0, (6,), 14)
+    gland(HB, 1, 11)
+    transposed(HB, 1, 0)
+    k_block(0, 3, False)
+    units(0)
+    gland(DYB, 0, 15)
+    gland(DYB, 0, 13)
+    gland(DYB, 0, 14)
     gh(1)
-    fwd(HB, 1, (0,), 5, 6)
-    fwd(HB, 1, (16,), 9)
     transposed(DYB, 0, 1)
-    fwd(HB, 1, (17,), 10)
-    fwd(HB, 1, (18,), 19, 20, 12)
-    fwd(HB, 1, (3, 4), 7, 11)
-    ready(HB, 1, 8, 9, 10)
-    units_a(0)
-    ready(HB, 1, 11)
-    transposed(HB, 1, 0)
-    units_b(0)
-    fwd(HB, 1, (5, 19), 13)
-    fwd(HB, 1, (6, 20), 14)
+    fwd(HB, 1, (6,), 14)
+    fwd(HB, 1, (5,), 13)
     fwd(HB, 1, (7,), 15)
-    ready(HB, 1, 12, 13, 14)
-    units_a(1)
-    ready(HB, 1, 15)
-    units_b(1)
+    gland(HB, 1, 14)
+    k_block(1, 2, False)
+    gland(HB, 1, 13)
+    k_block(1, 1, False)
+    gland(HB, 1, 15)
+    k_block(1, 3, False)
+    units(1)
     weights(0)
-    y_own(1, 2)
+    transposed(HB, 1, 1)
+    weights(2)
+    weights(4)
     y_sib(0, 0)
-    weights(1)
     y_own(0, 0)
-    step_bx2(0)
+    y_sib(0, 2)
+    y_sib(0, 1)
     y_merge(0, 0, V1P, V1M)
-    transposed(HB, 1, 1)
-    y_sib(1, 1)
-    weights(4)
-    y_sib(0, 2)
-    weights(3)
+    weights(5)
     step_ap(0)
-    y_sib(0, 1)
+    left_gather(HB, 1)
     y_own(0, 2)
     y_merge(0, 2, VIM)
-    y_relay(0, 1)
-    step_bx2(4)
+    weights(1)
     y_own(0, 1)
     y_merge(0, 1, VIP)
+    step_bx2(5)
+    y_own(1, 2)
+    y_sib(1, 3)
+    y_relay(0, 1)
+    step_ap(2)
+    y_own(1, 3)
+    step_bx2(2)
+    step_bx2(6)
     y_relay(0, 0)
-    weights(2)
-    step_bx2(3)
-    step_ap(1)
+    left_table(0)
     y_sib(1, 0)
-    step_bs(0)
+    y_sib(1, 1)
+    y_merge(1, 3)
     y_own(1, 0)
-    y_sib(1, 3)
+    step_ax1(0)
+    step_bx2(0)
+    y_own(1, 1)
+    y_sib(1, 2)
+    step_bx2(1)
+    y_merge(1, 0, V1P, V1M)
     y_sib(0, 3)
-    step_bs(4)
-    step_bx2(1)
-    y_own(1, 3)
-    y_sib(1, 2)
-    step_bx2(2)
-    y_merge(1, 0, V1P, V1M)
-    weights(5)
     step_ap(4)
-    step_ax1(1)
-    step_ax1(0)
-    y_own(1, 1)
     y_merge(1, 1, VIP)
+    step_ax1(2)
+    weights(3)
+    step_bs(5)
     y_merge(1, 2, VIM)
+    step_bx2(4)
     y_own(0, 3)
     y_merge(0, 3)
+    step_bs(2)
+    y_p(0)
+    left_gather(DYB, 0)
+    y_f(0)
+    step_bs(6)
+    step_ax2(0)
+    step_ax1(4)
+    step_ap(1)
+    step_bs(0)
+    y_relay(1, 1)
+    y_relay(1, 0)
+    step_bs(1)
+    step_ax2(2)
+    y_partial()
+    step_bx2(3)
+    step_ap(3)
+    step_ax1(1)
+    step_bp(5)
+    step_bs(4)
+    step_bp(2)
+    step_af(0)
+    left_a(0)
+    step_ax2(4)
+    step_bp(6)
+    y_p(1)
+    step_ax1(3)
+    y_f(1)
+    step_af(2)
+    left_a(2)
+    step_bp(0)
+    step_bf(5)
+    left_b(5)
+    step_bf(2)
+    left_b(2)
     step_bs(3)
-    y_merge(1, 3)
-    y_p(0)
-    step_bs(1)
-    y_f(0)
-    step_bs(2)
-    step_ax1(4)
-    step_bx2(5)
-    step_ap(3)
-    y_relay(1, 1)
-    step_bx2(6)
-    y_relay(1, 0)
-    y_partial()
+    step_bf(6)
+    step_bp(1)
+    left_b(6)
+    tmid(1)
     step_ax2(1)
-    step_ap(2)
-    step_ax2(0)
-    step_ax1(3)
-    step_bp(0)
-    step_ax2(4)
     step_bp(4)
-    y_p(1)
-    step_bs(5)
+    step_af(4)
+    left_a(4)
+    step_ax2(3)
     step_bp(3)
-    step_ax1(2)
-    y_f(1)
-    step_bs(6)
+    y_block_out()
+    left_sums(1)
     step_bf(0)
-    step_bp(1)
+    left_b(0)
     step_af(1)
+    left_a(1)
+    y_grad_tokens()
+    left_sums(0)
+    step_bf(1)
+    left_table(1)
+    step_af(3)
+    left_a(3)
+    left_b(1)
     step_bf(4)
-    step_af(0)
-    step_bp(2)
-    step_ax2(3)
-    tmid(1)
-    step_af(4)
-    step_bp(5)
-    step_ax2(2)
-    step_bp(6)
-    y_block_out()
-    step_af(3)
+    left_b(4)
     step_bf(3)
-    step_bf(1)
-    step_bf(2)
-    step_af(2)
-    y_grad_tokens()
-    step_bf(5)
-    step_bf(6)
-    for g, B in ((0, DYB), (1, HB)):
-        for k in range(21):
-            gcopy(B, g, k).wait_send()
-    for e in range(2):
-        for a in range(2):
-            for k in range(1, 4):
-                tcopy(e, a, k).wait_send()
-        for i in range(4):
-            sib_copy(e, i).wait_send()
-        for k in range(7):
-            y_copy(k, e).wait_send()
-    for k in range(8):
-        for a in range(len(A_PARTS)):
-            a_copy(k, a).wait_send()
-        for b in range(len(B_PARTS)):
-            b_copy(k, b).wait_send()
+    left_b(3)
 
 
 def emit(bo_ref, gt_ref, rn_ref, gg_ref, gr_ref, bo, gt, rn, gg, g_gate, g_up, g_down, sem):
@@ -721,9 +745,9 @@
         V((2, 4, 2 * ROWS, FEAT), BF16), V((2, 2, ROWS, FEAT), BF16),
         V((2, 2, 2 * ROWS, FEAT), BF16), V((2, ROWS, FEAT), BF16), V((2, ROWS, FEAT), BF16),
         V((2, ROWS, FEAT), F32),
-        dma((8,)), dma((2, 21)), dma((2, 21)), dma((2, 2, 4)), dma((2, 2, 4)),
-        dma((8, na)), dma((8, na)), dma((8, nb)), dma((8, nb)), dma((2, 7)), dma((2, 7)),
-        dma((2, 4)), dma((2, 4)),
+        dma((8,)), dma((2,)), dma((2, 18)), dma((2,)), dma((2, 2, 3)),
+        dma((na,)), dma((4, na)), dma((nb,)), dma((4, nb)), dma((2,)), dma((2, 5)),
+        dma((2,)), dma((2, 4)),
     ]
     held = (
         ((ROWS, FEAT), BF16), ((ROWS, FEAT), BF16), ((1, FEAT), F32), ((1, FEAT), F32),

time: 85.6 us -> 83.6 us (0.977)
  Pallas kernels: 83.5 us -> 81.6 us
    pallas_call x1, Pallas kernels: 82.2 us -> 80.2 us  [body(): pl.pallas_call(kernel, out_shape=tuple((pltpu.VMEM(shape, dtype) for shap...]
where the time goes in v4:
time: 83.6 us; the launch traced here: 82.4 us
  Pallas kernels  81.6 us (98%)
    pallas_call x1, Pallas kernels, body(): pl.pallas_call(kernel, out_shape=tuple((pltpu.VMEM(shape, dtype) for shap...  80.2 us

profile of v4, /device:TPU:32, one launch (start us, length us, event | category | flops | bytes accessed | tf_op | source)
XLA Modules:
  0.0 82.4 jit_solution(10374935857502943950)
XLA Ops:
  0.6 80.2 %shard_map.135 = (bf16[384,256]{1,0:T(8,128)(2,1)S(1)}, bf16[384,256]{1,0:T(8,128)(2,1)S(1)}, f32[1,256]{1,0:T(1,128)S(1)}, f32[1,256]{1,0:T(1,128)S(1)}, f32[3,128,1024]{2,1,0:T(8,128)S(1)}) custom-call(bf16[384,256]{1,0:T(8,128)(2,1)} %tok_hbm.1, f32[1,2048]{1,0:T(1,128)} %bitcast.5, f32[1,256]{1,0:T(1,128)} %bitcast.6, bf16[2048,1024]{1,0:T(8,128)(2,1)} %gw_hbm.1, ...), custom_call_target="tpu_custom_call" | custom-call | tf_op jit(solution)/shard_map/pallas_call | solution.py:756
  80.9 1.3 %shard_map.136 = (bf16[384,256]{1,0:T(8,128)(2,1)}, bf16[384,256]{1,0:T(8,128)(2,1)}, f32[1,256]{1,0:T(1,128)}, f32[1,256]{1,0:T(1,128)}, f32[128,1024]{1,0:T(8,...) custom-call(bf16[384,256]{1,0:T(8,128)(2,1)S(1)} %get-tuple-element.19.bo_ref, ...), custom_call_target="tpu_custom_call" | custom-call | tf_op jit(solution)/shard_map/pallas_call | solution.py:770

commit v5 on v4

--- a/solution.py
+++ b/solution.py
@@ -246,6 +246,25 @@
             G[1, ro, :] = (gh * lift * sigma * (1.0 + gate * (1.0 - sigma))).astype(BF16)
             G[2, ro, :] = (gh * gate * sigma).astype(BF16)
 
+    def k_half(slot, i, sib, first):
+        cc = 1 - c if sib else c
+        ks = pl.ds(pl.multiple_of(((y, ym, yp, y2)[i] * 2 + cc) * FEAT, FEAT), FEAT)
+        for wi, dst in ((0, GT), (1, LF)):
+            v = jnp.dot(HB[slot, :, ks], W[wi, ks, :], preferred_element_type=F32)
+            dst[slot] = v if first else dst[slot] + v
+
+    def gh_block(i, first):
+        yy = (y, ym, yp, y2)[i]
+        ks = pl.ds(pl.multiple_of(yy * 2 * FEAT, 2 * FEAT), 2 * FEAT)
+        v = jnp.dot(DYB[1, :, ks], W[2, ks, :], preferred_element_type=F32)
+        GH[1] = v if first else GH[1] + v
+
+    def tx_block(B, n, slot, i):
+        yy = (y, ym, yp, y2)[i]
+        for h in range(2):
+            cols = pl.ds(pl.multiple_of((yy * 2 + h) * FEAT, FEAT), FEAT)
+            LT[n, cols, pl.ds(slot * ROWS, ROWS)] = B[slot, :, cols].T
+
     def gh(slot):
         if slot == 0:
             cp_w[2].wait()
@@ -330,6 +349,39 @@
                     for k in ks:
                         b_copy(k, B_PARTS.index((p, off))).start()
 
+    def weights_first(p):
+        mi, j = p // 2, p % 2
+
+        @pl.loop(0, 4)
+        def _(n):
+            xd = (x + 2 + n) % 4
+            blocks = [pl.multiple_of(zd * HALF + xd * 128, 128) for zd in range(4)]
+            lhs = jnp.concatenate(
+                [LT[(mi + 1) // 2, pl.ds(r, 128), :] for r in blocks], axis=0
+            )
+            res = jnp.dot(
+                lhs, G[mi, :, j * 256 : (j + 1) * 256], preferred_element_type=F32
+            ).astype(BF16)
+            for off in range(2):
+                for zd in range(4):
+                    part = res[zd * 128 : (zd + 1) * 128, off * 128 : (off + 1) * 128]
+                    if (p, off) in A_PARTS:
+                        PA[A_PARTS.index((p, off)), pl.ds(blocks[zd], 128), :] = part
+                    else:
+                        PB[B_PARTS.index((p, off)), xd, zd] = part
+            for at, ks in ((0, (BX1P, BX1M)), (1, (BXIM,)), (3, (BXIP,))):
+
+                @pl.when(n == at)
+                def _():
+                    for k in ks:
+                        for off in range(2):
+                            if (p, off) in B_PARTS:
+                                b_copy(k, B_PARTS.index((p, off))).start()
+
+        for off in range(2):
+            if (p, off) in A_PARTS:
+                a_copy(AS, A_PARTS.index((p, off))).start()
+
     def plus(a, b):
         return a.astype(F32) + b.astype(F32)
 
@@ -551,161 +603,170 @@
     fwd(DYB, 0, (16,), 9)
     fwd(DYB, 0, (17,), 10)
     stat2()
+    gland(DYB, 0, 9)
     gland(DYB, 0, 8)
-    fwd(DYB, 0, (3,), 7, 11)
-    gland(DYB, 0, 9)
     gland(DYB, 0, 10)
     gland(HB, 1, 8)
+    fwd(DYB, 0, (3,), 7, 11)
     k_block(0, 0, True)
     gland(DYB, 0, 11)
-    transposed(DYB, 0, 0)
     gh(0)
     fwd(HB, 1, (1,), 3)
     fwd(HB, 1, (2,), 4)
     fwd(DYB, 0, (18,), 19, 20, 12)
     fwd(HB, 1, (0,), 5, 6)
+    transposed(DYB, 0, 0)
     gland(DYB, 0, 12)
+    fwd(HB, 1, (16,), 9)
+    fwd(HB, 1, (17,), 10)
     fwd(HB, 1, (18,), 19, 20, 12)
-    fwd(HB, 1, (17,), 10)
-    fwd(HB, 1, (16,), 9)
+    tx_block(DYB, 0, 1, 0)
+    gh_block(0, True)
+    gland(HB, 1, 9)
     gland(HB, 1, 12)
     k_block(1, 0, True)
+    fwd(HB, 1, (3,), 7, 11)
     gland(HB, 1, 10)
-    k_block(0, 2, False)
-    fwd(HB, 1, (3,), 7, 11)
-    gland(HB, 1, 9)
     k_block(0, 1, False)
     fwd(DYB, 0, (7,), 15)
+    k_block(0, 2, False)
+    gland(HB, 1, 11)
     fwd(DYB, 0, (5,), 13)
     fwd(DYB, 0, (6,), 14)
-    gland(HB, 1, 11)
-    transposed(HB, 1, 0)
     k_block(0, 3, False)
     units(0)
     gland(DYB, 0, 15)
+    transposed(HB, 1, 0)
+    gland(DYB, 0, 14)
+    gh_block(2, False)
     gland(DYB, 0, 13)
-    gland(DYB, 0, 14)
-    gh(1)
-    transposed(DYB, 0, 1)
+    tx_block(DYB, 0, 1, 1)
+    gh_block(3, False)
+    tx_block(DYB, 0, 1, 2)
+    gh_block(1, False)
+    tx_block(DYB, 0, 1, 3)
+    fwd(HB, 1, (5,), 13)
     fwd(HB, 1, (6,), 14)
-    fwd(HB, 1, (5,), 13)
+    k_half(1, 2, False, False)
     fwd(HB, 1, (7,), 15)
+    k_half(1, 1, False, False)
+    k_half(1, 3, False, False)
+    gland(HB, 1, 13)
+    k_half(1, 1, True, False)
     gland(HB, 1, 14)
-    k_block(1, 2, False)
-    gland(HB, 1, 13)
-    k_block(1, 1, False)
+    k_half(1, 2, True, False)
     gland(HB, 1, 15)
-    k_block(1, 3, False)
+    k_half(1, 3, True, False)
     units(1)
+    weights_first(1)
     weights(0)
+    y_sib(0, 0)
     transposed(HB, 1, 1)
+    left_gather(HB, 1)
+    weights(5)
+    left_gather(DYB, 0)
+    left_table(0)
+    y_own(0, 0)
+    y_merge(0, 0, V1P, V1M)
+    y_sib(0, 2)
+    y_sib(1, 0)
+    y_own(0, 2)
+    weights(4)
+    y_merge(0, 2, VIM)
+    step_bx2(0)
+    y_sib(0, 1)
     weights(2)
-    weights(4)
-    y_sib(0, 0)
-    y_own(0, 0)
-    y_sib(0, 2)
-    y_sib(0, 1)
-    y_merge(0, 0, V1P, V1M)
-    weights(5)
-    step_ap(0)
-    left_gather(HB, 1)
-    y_own(0, 2)
-    y_merge(0, 2, VIM)
-    weights(1)
+    step_bx2(5)
     y_own(0, 1)
     y_merge(0, 1, VIP)
-    step_bx2(5)
+    step_ap(1)
+    step_bx2(1)
+    y_own(1, 0)
+    y_relay(0, 1)
+    y_own(1, 3)
+    y_sib(1, 3)
+    y_sib(1, 1)
+    y_own(1, 1)
+    step_ap(0)
+    y_merge(1, 0, V1P, V1M)
+    y_sib(1, 2)
+    y_relay(0, 0)
+    y_sib(0, 3)
+    weights(3)
+    step_ap(4)
+    step_bs(0)
     y_own(1, 2)
-    y_sib(1, 3)
-    y_relay(0, 1)
-    step_ap(2)
-    y_own(1, 3)
+    y_merge(1, 3)
     step_bx2(2)
-    step_bx2(6)
-    y_relay(0, 0)
-    left_table(0)
-    y_sib(1, 0)
-    y_sib(1, 1)
-    y_merge(1, 3)
-    y_own(1, 0)
-    step_ax1(0)
-    step_bx2(0)
-    y_own(1, 1)
-    y_sib(1, 2)
-    step_bx2(1)
-    y_merge(1, 0, V1P, V1M)
-    y_sib(0, 3)
-    step_ap(4)
-    y_merge(1, 1, VIP)
-    step_ax1(2)
-    weights(3)
-    step_bs(5)
-    y_merge(1, 2, VIM)
-    step_bx2(4)
     y_own(0, 3)
     y_merge(0, 3)
+    step_ax1(1)
+    y_merge(1, 2, VIM)
+    y_p(0)
+    y_merge(1, 1, VIP)
+    step_bs(5)
+    y_relay(1, 0)
+    step_bx2(4)
+    step_bx2(3)
+    step_ap(2)
+    step_bx2(6)
+    step_ax1(4)
+    step_ax1(0)
+    y_relay(1, 1)
     step_bs(2)
-    y_p(0)
-    left_gather(DYB, 0)
     y_f(0)
+    step_ax2(1)
+    y_partial()
+    step_ap(3)
+    step_bs(3)
+    step_bs(4)
+    step_bp(0)
+    step_bp(5)
+    step_ax1(2)
+    step_ax2(4)
     step_bs(6)
-    step_ax2(0)
-    step_ax1(4)
-    step_ap(1)
-    step_bs(0)
-    y_relay(1, 1)
-    y_relay(1, 0)
     step_bs(1)
-    step_ax2(2)
-    y_partial()
-    step_bx2(3)
-    step_ap(3)
-    step_ax1(1)
-    step_bp(5)
-    step_bs(4)
     step_bp(2)
-    step_af(0)
-    left_a(0)
-    step_ax2(4)
-    step_bp(6)
     y_p(1)
     step_ax1(3)
+    step_ax2(0)
     y_f(1)
-    step_af(2)
-    left_a(2)
-    step_bp(0)
+    tmid(1)
+    step_bp(3)
     step_bf(5)
+    step_af(1)
+    step_bf(2)
+    step_af(4)
     left_b(5)
-    step_bf(2)
-    left_b(2)
-    step_bs(3)
-    step_bf(6)
-    step_bp(1)
-    left_b(6)
-    tmid(1)
-    step_ax2(1)
+    step_bp(6)
     step_bp(4)
-    step_af(4)
-    left_a(4)
-    step_ax2(3)
-    step_bp(3)
-    y_block_out()
-    left_sums(1)
+    step_ax2(2)
     step_bf(0)
     left_b(0)
-    step_af(1)
+    step_ax2(3)
+    step_bp(1)
+    left_b(2)
     left_a(1)
+    left_a(4)
+    step_af(0)
+    step_bf(3)
     y_grad_tokens()
+    left_a(0)
+    step_af(2)
+    y_block_out()
+    left_b(3)
     left_sums(0)
-    step_bf(1)
     left_table(1)
+    left_a(2)
+    step_bf(6)
+    step_bf(4)
+    left_sums(1)
+    left_b(4)
+    left_b(6)
     step_af(3)
     left_a(3)
+    step_bf(1)
     left_b(1)
-    step_bf(4)
-    left_b(4)
-    step_bf(3)
-    left_b(3)
 
 
 def emit(bo_ref, gt_ref, rn_ref, gg_ref, gr_ref, bo, gt, rn, gg, g_gate, g_up, g_down, sem):

time: 83.6 us -> 82.6 us (0.988)
  no operation moved by 1% of the time
where the time goes in v5:
time: 82.6 us; the launch traced here: 82.1 us
  Pallas kernels  81.3 us (98%)
    pallas_call x1, Pallas kernels, body(): pl.pallas_call(kernel, out_shape=tuple((pltpu.VMEM(shape, dtype) for shap...  79.9 us

profile of v5, /device:TPU:32, one launch (start us, length us, event | category | flops | bytes accessed | tf_op | source)
XLA Modules:
  0.0 82.1 jit_solution(7769568848585999502)
XLA Ops:
  0.6 79.9 %shard_map.135 = (bf16[384,256]{1,0:T(8,128)(2,1)S(1)}, bf16[384,256]{1,0:T(8,128)(2,1)S(1)}, f32[1,256]{1,0:T(1,128)S(1)}, f32[1,256]{1,0:T(1,128)S(1)}, f32[3,128,1024]{2,1,0:T(8,128)S(1)}) custom-call(bf16[384,256]{1,0:T(8,128)(2,1)} %tok_hbm.1, f32[1,2048]{1,0:T(1,128)} %bitcast.5, f32[1,256]{1,0:T(1,128)} %bitcast.6, bf16[2048,1024]{1,0:T(8,128)(2,1)} %gw_hbm.1, ...), custom_call_target="tpu_custom_call" | custom-call | tf_op jit(solution)/shard_map/pallas_call | solution.py:817
  80.6 1.3 %shard_map.136 = (bf16[384,256]{1,0:T(8,128)(2,1)}, bf16[384,256]{1,0:T(8,128)(2,1)}, f32[1,256]{1,0:T(1,128)}, f32[1,256]{1,0:T(1,128)}, f32[128,1024]{1,0:T(8,...) custom-call(bf16[384,256]{1,0:T(8,128)(2,1)S(1)} %get-tuple-element.19.bo_ref, ...), custom_call_target="tpu_custom_call" | custom-call | tf_op jit(solution)/shard_map/pallas_call | solution.py:831

commit v6 on v5

--- a/solution.py
+++ b/solution.py
@@ -599,58 +599,58 @@
     tmid(0)
     fwd(DYB, 0, (2,), 4)
     fwd(DYB, 0, (1,), 3)
+    fwd(DYB, 0, (16,), 9)
     fwd(DYB, 0, (0,), 5, 6)
-    fwd(DYB, 0, (16,), 9)
+    stat2()
+    gland(DYB, 0, 8)
+    gland(DYB, 0, 9)
     fwd(DYB, 0, (17,), 10)
-    stat2()
-    gland(DYB, 0, 9)
-    gland(DYB, 0, 8)
+    fwd(DYB, 0, (3,), 7, 11)
+    gland(HB, 1, 8)
+    gland(DYB, 0, 11)
     gland(DYB, 0, 10)
-    gland(HB, 1, 8)
-    fwd(DYB, 0, (3,), 7, 11)
-    k_block(0, 0, True)
-    gland(DYB, 0, 11)
+    transposed(DYB, 0, 0)
     gh(0)
     fwd(HB, 1, (1,), 3)
     fwd(HB, 1, (2,), 4)
     fwd(DYB, 0, (18,), 19, 20, 12)
     fwd(HB, 1, (0,), 5, 6)
-    transposed(DYB, 0, 0)
     gland(DYB, 0, 12)
-    fwd(HB, 1, (16,), 9)
     fwd(HB, 1, (17,), 10)
-    fwd(HB, 1, (18,), 19, 20, 12)
     tx_block(DYB, 0, 1, 0)
     gh_block(0, True)
+    k_block(0, 0, True)
+    fwd(HB, 1, (16,), 9)
+    fwd(HB, 1, (18,), 19, 20, 12)
+    fwd(HB, 1, (3,), 7, 11)
+    gland(HB, 1, 10)
     gland(HB, 1, 9)
     gland(HB, 1, 12)
     k_block(1, 0, True)
-    fwd(HB, 1, (3,), 7, 11)
-    gland(HB, 1, 10)
+    k_block(0, 2, False)
+    fwd(DYB, 0, (7,), 15)
+    fwd(DYB, 0, (5,), 13)
+    gland(HB, 1, 11)
+    fwd(DYB, 0, (6,), 14)
+    transposed(HB, 1, 0)
     k_block(0, 1, False)
-    fwd(DYB, 0, (7,), 15)
-    k_block(0, 2, False)
-    gland(HB, 1, 11)
-    fwd(DYB, 0, (5,), 13)
-    fwd(DYB, 0, (6,), 14)
+    gland(DYB, 0, 15)
     k_block(0, 3, False)
-    units(0)
-    gland(DYB, 0, 15)
-    transposed(HB, 1, 0)
     gland(DYB, 0, 14)
-    gh_block(2, False)
     gland(DYB, 0, 13)
     tx_block(DYB, 0, 1, 1)
-    gh_block(3, False)
-    tx_block(DYB, 0, 1, 2)
     gh_block(1, False)
     tx_block(DYB, 0, 1, 3)
+    units(0)
+    gh_block(2, False)
     fwd(HB, 1, (5,), 13)
     fwd(HB, 1, (6,), 14)
+    k_half(1, 1, False, False)
+    gh_block(3, False)
+    fwd(HB, 1, (7,), 15)
+    tx_block(DYB, 0, 1, 2)
+    k_half(1, 3, False, False)
     k_half(1, 2, False, False)
-    fwd(HB, 1, (7,), 15)
-    k_half(1, 1, False, False)
-    k_half(1, 3, False, False)
     gland(HB, 1, 13)
     k_half(1, 1, True, False)
     gland(HB, 1, 14)
@@ -658,115 +658,115 @@
     gland(HB, 1, 15)
     k_half(1, 3, True, False)
     units(1)
-    weights_first(1)
-    weights(0)
+    weights_first(0)
+    weights(1)
+    left_gather(HB, 1)
+    left_table(0)
+    left_gather(DYB, 0)
+    transposed(HB, 1, 1)
     y_sib(0, 0)
-    transposed(HB, 1, 1)
-    left_gather(HB, 1)
     weights(5)
-    left_gather(DYB, 0)
-    left_table(0)
     y_own(0, 0)
     y_merge(0, 0, V1P, V1M)
     y_sib(0, 2)
+    weights(4)
+    y_own(0, 2)
     y_sib(1, 0)
-    y_own(0, 2)
-    weights(4)
     y_merge(0, 2, VIM)
+    y_own(0, 1)
+    y_sib(0, 1)
+    step_bx2(1)
+    step_ap(0)
+    weights(2)
+    y_sib(0, 3)
+    y_merge(0, 1, VIP)
+    y_relay(0, 1)
     step_bx2(0)
-    y_sib(0, 1)
-    weights(2)
     step_bx2(5)
-    y_own(0, 1)
-    y_merge(0, 1, VIP)
-    step_ap(1)
-    step_bx2(1)
-    y_own(1, 0)
-    y_relay(0, 1)
-    y_own(1, 3)
     y_sib(1, 3)
     y_sib(1, 1)
+    step_ap(1)
     y_own(1, 1)
-    step_ap(0)
+    step_bx2(4)
+    y_own(1, 0)
+    y_relay(0, 0)
+    y_own(0, 3)
     y_merge(1, 0, V1P, V1M)
+    y_own(1, 3)
+    y_merge(1, 3)
+    y_own(1, 2)
+    step_ap(4)
+    y_merge(0, 3)
     y_sib(1, 2)
-    y_relay(0, 0)
-    y_sib(0, 3)
+    step_bx2(2)
     weights(3)
-    step_ap(4)
+    y_p(0)
+    step_ax1(0)
+    step_ax1(1)
+    step_bx2(6)
+    y_merge(1, 2, VIM)
+    y_merge(1, 1, VIP)
     step_bs(0)
-    y_own(1, 2)
-    y_merge(1, 3)
-    step_bx2(2)
-    y_own(0, 3)
-    y_merge(0, 3)
-    step_ax1(1)
-    y_merge(1, 2, VIM)
-    y_p(0)
-    y_merge(1, 1, VIP)
+    step_ap(2)
+    y_f(0)
     step_bs(5)
-    y_relay(1, 0)
-    step_bx2(4)
-    step_bx2(3)
-    step_ap(2)
-    step_bx2(6)
-    step_ax1(4)
-    step_ax1(0)
     y_relay(1, 1)
     step_bs(2)
-    y_f(0)
-    step_ax2(1)
+    step_bs(4)
+    step_bs(1)
+    step_ax1(4)
     y_partial()
     step_ap(3)
-    step_bs(3)
-    step_bs(4)
+    step_bx2(3)
+    y_relay(1, 0)
+    step_ax2(0)
     step_bp(0)
+    step_ax2(1)
     step_bp(5)
     step_ax1(2)
+    step_bs(6)
     step_ax2(4)
-    step_bs(6)
-    step_bs(1)
     step_bp(2)
     y_p(1)
     step_ax1(3)
-    step_ax2(0)
+    step_bp(4)
+    step_bs(3)
+    step_bp(1)
+    step_af(0)
+    step_bf(0)
+    step_af(1)
+    tmid(1)
+    step_bf(5)
+    left_a(0)
+    left_b(0)
+    left_a(1)
+    left_b(5)
+    step_ax2(2)
+    step_bp(6)
     y_f(1)
-    tmid(1)
+    step_af(4)
+    step_ax2(3)
     step_bp(3)
-    step_bf(5)
-    step_af(1)
     step_bf(2)
-    step_af(4)
-    left_b(5)
-    step_bp(6)
-    step_bp(4)
-    step_ax2(2)
-    step_bf(0)
-    left_b(0)
-    step_ax2(3)
-    step_bp(1)
+    y_grad_tokens()
+    left_sums(0)
+    left_a(4)
+    y_block_out()
+    left_sums(1)
+    step_af(2)
+    left_table(1)
+    step_bf(4)
+    left_b(4)
     left_b(2)
-    left_a(1)
-    left_a(4)
-    step_af(0)
-    step_bf(3)
-    y_grad_tokens()
-    left_a(0)
-    step_af(2)
-    y_block_out()
-    left_b(3)
-    left_sums(0)
-    left_table(1)
+    step_bf(1)
     left_a(2)
     step_bf(6)
-    step_bf(4)
-    left_sums(1)
-    left_b(4)
+    left_b(1)
     left_b(6)
     step_af(3)
     left_a(3)
-    step_bf(1)
-    left_b(1)
+    step_bf(3)
+    left_b(3)
 
 
 def emit(bo_ref, gt_ref, rn_ref, gg_ref, gr_ref, bo, gt, rn, gg, g_gate, g_up, g_down, sem):

time: 82.6 us -> 82.5 us (level)
  no operation moved by 1% of the time
where the time goes in v6:
time: 82.5 us; the launch traced here: 82.2 us
  Pallas kernels  81.4 us (99%)
    pallas_call x1, Pallas kernels, body(): pl.pallas_call(kernel, out_shape=tuple((pltpu.VMEM(shape, dtype) for shap...  80.1 us

profile of v6, /device:TPU:32, one launch (start us, length us, event | category | flops | bytes accessed | tf_op | source)
XLA Modules:
  0.0 82.2 jit_solution(4269993582910768736)
XLA Ops:
  0.6 80.1 %shard_map.135 = (bf16[384,256]{1,0:T(8,128)(2,1)S(1)}, bf16[384,256]{1,0:T(8,128)(2,1)S(1)}, f32[1,256]{1,0:T(1,128)S(1)}, f32[1,256]{1,0:T(1,128)S(1)}, f32[3,128,1024]{2,1,0:T(8,128)S(1)}) custom-call(bf16[384,256]{1,0:T(8,128)(2,1)} %tok_hbm.1, f32[1,2048]{1,0:T(1,128)} %bitcast.5, f32[1,256]{1,0:T(1,128)} %bitcast.6, bf16[2048,1024]{1,0:T(8,128)(2,1)} %gw_hbm.1, ...), custom_call_target="tpu_custom_call" | custom-call | tf_op jit(solution)/shard_map/pallas_call | solution.py:817
  80.8 1.3 %shard_map.136 = (bf16[384,256]{1,0:T(8,128)(2,1)}, bf16[384,256]{1,0:T(8,128)(2,1)}, f32[1,256]{1,0:T(1,128)}, f32[1,256]{1,0:T(1,128)}, f32[128,1024]{1,0:T(8,...) custom-call(bf16[384,256]{1,0:T(8,128)(2,1)S(1)} %get-tuple-element.19.bo_ref, ...), custom_call_target="tpu_custom_call" | custom-call | tf_op jit(solution)/shard_map/pallas_call | solution.py:831
